TPU v7x, 32 devices: a whole 2x2x4 slice. The times are simulated.
32 devices in a mesh: dp: 8 (over z, y), tensor: 4 (over x, core).
Axes of the slice: x: 2, y: 2, z: 4, core: 2. Of those that a mesh axis runs over, the one named last changes fastest.
Arguments:
- layer_in: bfloat16 [24576, 768], P(('dp', 'tensor')), may hold values from -6 to 6
- prompt_len: int32 [8], P('dp'), may hold values from 512 to 1024, as said below
- cont_len: int32 [8, 8], P('dp'), may hold values from 128 to 256, as said below
- w_qkv: bfloat16 [3, 768, 768], P(None, None, 'tensor'), may hold values from -0.21875 to 0.21875
- b_qv: bfloat16 [2, 768], P(None, 'tensor'), may hold values from -3 to 3
- w_proj: bfloat16 [768, 768], P('tensor'), may hold values from -1.75 to 1.75
- b_proj: bfloat16 [768], replicated, may hold values from -2 to 2
- ln1_gain: bfloat16 [768], replicated, may hold values from 0.25 to 1.75
- ln1_bias: bfloat16 [768], replicated, may hold values from -2 to 2
- ln2_gain: bfloat16 [768], replicated, may hold values from 0.25 to 1.75
- ln2_bias: bfloat16 [768], replicated, may hold values from -2 to 2
- w_in: bfloat16 [768, 3072], P(None, 'tensor'), may hold values from -0.21875 to 0.21875
- b_in: bfloat16 [3072], P('tensor'), may hold values from -2 to 2
- w_out: bfloat16 [3072, 768], P('tensor'), may hold values from -0.109375 to 0.109375
- b_out: bfloat16 [768], replicated, may hold values from -2 to 2
- out_grad: bfloat16 [24576, 768], P(('dp', 'tensor')), may hold values from -6 to 6
Outputs:
- layer_out: bfloat16 [24576, 768], P(('dp', 'tensor'))
- in_grad: float32 [24576, 768], P(('dp', 'tensor'))
- grad_w_qkv: float32 [3, 768, 768], P(None, None, 'tensor')
- grad_b_qv: float32 [2, 768], P(None, 'tensor')
- grad_w_proj: float32 [768, 768], P('tensor')
- grad_b_proj: float32 [768], replicated
- grad_ln1_gain: float32 [768], replicated
- grad_ln1_bias: float32 [768], replicated
- grad_ln2_gain: float32 [768], replicated
- grad_ln2_bias: float32 [768], replicated
- grad_w_in: float32 [768, 3072], P(None, 'tensor')
- grad_b_in: float32 [3072], P('tensor')
- grad_w_out: float32 [3072, 768], P('tensor')
- grad_b_out: float32 [768], replicated
Inputs may be any that keep to these rules, and one draw needn't show every extreme that they name: `prompt_len`: in every draw some group's prompt has all 1024 rows valid. `cont_len`: in every group some continuation has all 256 rows valid.
All inputs are finite; a program needn't handle non-finite values.
Results may differ from a plain program's by a relative error of at most 0.018.
Values may be sent and summed in bfloat16 or wider, within the bound.
A program may use at most 192 MiB of HBM per device.

v0:
```python
import jax
import jax.numpy as jnp
from jax import lax
from jax.sharding import PartitionSpec as P

HEAD = 64
PROMPT = 1024
CONT = 8
CLEN = 256


epsilon = 1e-06
masked_score = -1000000000.0


def layer_norm(values, gain, shift):
    mean_row = jnp.mean(values, axis=-1, keepdims=True)
    centred = values - mean_row
    spread = jnp.mean(centred * centred, axis=-1, keepdims=True)
    return centred * lax.rsqrt(spread + epsilon) * gain + shift


def exact_gelu(values):
    return jax.nn.gelu(values, approximate=False)


def block_scores(queries, key_rows, allowed):
    scores = (
        jnp.einsum("bqhe,bkhe->bhqk", queries, key_rows, preferred_element_type=jnp.float32) * 0.125
    )
    return jnp.where(allowed[:, None, None, :], scores, masked_score)


def forward_block(queries, key_rows, value_rows, allowed):
    scores = block_scores(queries, key_rows, allowed)
    row_max = jnp.max(scores, axis=-1, keepdims=True)
    exponent = jnp.exp(scores - row_max)
    totals = jnp.sum(exponent, axis=-1, keepdims=True)
    prob_low = (exponent / totals).astype(jnp.bfloat16)
    context = jnp.einsum(
        "bhqk,bkhe->bqhe", prob_low, value_rows, preferred_element_type=jnp.float32
    )
    return (context, row_max + jnp.log(totals))


def backward_block(queries, key_rows, value_rows, allowed, log_total, grad_ctx):
    attn_prob = jnp.exp(block_scores(queries, key_rows, allowed) - log_total)
    grad_prob = jnp.einsum(
        "bqhe,bkhe->bhqk", grad_ctx, value_rows, preferred_element_type=jnp.float32
    )
    row_inner = jnp.sum(attn_prob * grad_prob, axis=-1, keepdims=True)
    grad_scores = (attn_prob * (grad_prob - row_inner)).astype(jnp.bfloat16)
    grad_query = (
        jnp.einsum("bhqk,bkhe->bqhe", grad_scores, key_rows, preferred_element_type=jnp.float32)
        * 0.125
    )
    grad_keys = (
        jnp.einsum("bhqk,bqhe->bkhe", grad_scores, queries, preferred_element_type=jnp.float32)
        * 0.125
    )
    grad_values = jnp.einsum(
        "bhqk,bqhe->bkhe",
        attn_prob.astype(jnp.bfloat16),
        grad_ctx,
        preferred_element_type=jnp.float32,
    )
    return (grad_query, grad_keys, grad_values)


def pair_keys(prompt_part, own_part):
    return jnp.concatenate(
        [jnp.broadcast_to(prompt_part, (2,) + prompt_part.shape[1:]), own_part], axis=1
    )


def pair_mask(prompt_valid, own_valid):
    return jnp.concatenate([jnp.broadcast_to(prompt_valid[None], (2, PROMPT)), own_valid], axis=1)


def contract_last(left, right):
    return lax.dot_general(
        left, right, (((1,), (1,)), ((), ())), preferred_element_type=jnp.float32
    )


def shards(
    layer_in,
    prompt_len,
    cont_len,
    w_qkv,
    b_qv,
    w_proj,
    b_proj,
    ln1_gain,
    ln1_bias,
    ln2_gain,
    ln2_bias,
    w_in,
    b_in,
    w_out,
    b_out,
    out_grad,
):
    local_rows = layer_in.shape[0]
    width_here = w_qkv.shape[2]
    heads = width_here // HEAD
    total_rows = local_rows * lax.axis_size("tensor")
    block_rows = min(512, PROMPT)
    blocks = PROMPT // block_rows
    pair_count = CONT // 2
    rows_in = layer_in.astype(jnp.float32)
    attn_norm, norm1_pull = jax.vjp(
        layer_norm, rows_in, ln1_gain.astype(jnp.float32), ln1_bias.astype(jnp.float32)
    )
    attn_input = attn_norm.astype(jnp.bfloat16)
    attn_input_all = lax.all_gather(attn_input, "tensor", axis=0, tiled=True)
    projected = jnp.einsum("rd,sdf->rsf", attn_input_all, w_qkv, preferred_element_type=jnp.float32)
    bias_rows = b_qv.astype(jnp.float32)
    queries = (projected[:, 0] + bias_rows[0]).astype(jnp.bfloat16).reshape(total_rows, heads, HEAD)
    key_rows = projected[:, 1].astype(jnp.bfloat16).reshape(total_rows, heads, HEAD)
    value_rows = (
        (projected[:, 2] + bias_rows[1]).astype(jnp.bfloat16).reshape(total_rows, heads, HEAD)
    )
    prompt_valid = jnp.arange(PROMPT) < prompt_len[0]
    own_valid = (jnp.arange(CLEN)[None, :] < cont_len[0][:, None]).reshape(pair_count, 2, CLEN)
    prompt_keys = key_rows[:PROMPT][None]
    prompt_values = value_rows[:PROMPT][None]
    prompt_queries = queries[:PROMPT].reshape(blocks, 1, block_rows, heads, HEAD)

    def cont_rows(whole):
        return whole[PROMPT:].reshape(pair_count, 2, CLEN, heads, HEAD)

    cont_queries = cont_rows(queries)
    cont_keys = cont_rows(key_rows)
    cont_values = cont_rows(value_rows)

    def prompt_forward(block_query):
        return forward_block(block_query, prompt_keys, prompt_values, prompt_valid[None])

    prompt_ctx, prompt_logs = lax.map(prompt_forward, prompt_queries)

    def pair_forward(pieces):
        block_query, own_keys, own_values, own_mask = pieces
        return forward_block(
            block_query,
            pair_keys(prompt_keys, own_keys),
            pair_keys(prompt_values, own_values),
            pair_mask(prompt_valid, own_mask),
        )

    pair_ctx, pair_logs = lax.map(pair_forward, (cont_queries, cont_keys, cont_values, own_valid))
    context = jnp.concatenate(
        [prompt_ctx.reshape(PROMPT, width_here), pair_ctx.reshape(CONT * CLEN, width_here)], axis=0
    ).astype(jnp.bfloat16)
    attn_out = lax.psum_scatter(
        jnp.dot(context, w_proj, preferred_element_type=jnp.float32).astype(jnp.bfloat16),
        "tensor",
        scatter_dimension=0,
        tiled=True,
    ).astype(jnp.float32) + b_proj.astype(jnp.float32)
    hidden = rows_in + attn_out
    mlp_norm, norm2_pull = jax.vjp(
        layer_norm, hidden, ln2_gain.astype(jnp.float32), ln2_bias.astype(jnp.float32)
    )
    mlp_input = mlp_norm.astype(jnp.bfloat16)
    grad_out = out_grad.astype(jnp.float32)
    mlp_input_all = lax.all_gather(mlp_input, "tensor", axis=0, tiled=True)
    pre_act = jnp.dot(mlp_input_all, w_in, preferred_element_type=jnp.float32) + b_in.astype(
        jnp.float32
    )
    gelu_out, gelu_pull = jax.vjp(exact_gelu, pre_act)
    gelu_rows = gelu_out.astype(jnp.bfloat16)
    branch = lax.psum_scatter(
        jnp.dot(gelu_rows, w_out, preferred_element_type=jnp.float32).astype(jnp.bfloat16),
        "tensor",
        scatter_dimension=0,
        tiled=True,
    ).astype(jnp.float32)
    out_grad_all = lax.all_gather(out_grad, "tensor", axis=0, tiled=True)
    grad_gelu = contract_last(out_grad_all, w_out)
    grad_pre = gelu_pull(grad_gelu)[0].astype(jnp.bfloat16)
    grad_w_out = jnp.einsum(
        "rf,rd->fd", gelu_rows, out_grad_all, preferred_element_type=jnp.float32
    )
    grad_w_in = jnp.einsum("rd,rf->df", mlp_input_all, grad_pre, preferred_element_type=jnp.float32)
    grad_b_in = jnp.sum(grad_pre.astype(jnp.float32), axis=0)
    grad_mlp_in = lax.psum_scatter(
        contract_last(grad_pre, w_in).astype(jnp.bfloat16),
        "tensor",
        scatter_dimension=0,
        tiled=True,
    ).astype(jnp.float32)
    layer_out = (hidden + (branch + b_out.astype(jnp.float32))).astype(jnp.bfloat16)
    hidden_back, grad_ln2_gain, grad_ln2_bias = norm2_pull(grad_mlp_in)
    grad_hidden = grad_out + hidden_back
    grad_attn = grad_hidden.astype(jnp.bfloat16)
    grad_b_proj = jnp.sum(grad_attn.astype(jnp.float32), axis=0)
    grad_b_out = jnp.sum(grad_out, axis=0)
    grad_attn_all = lax.all_gather(grad_attn, "tensor", axis=0, tiled=True)
    grad_w_proj = jnp.einsum(
        "rf,rd->fd", context, grad_attn_all, preferred_element_type=jnp.float32
    )
    grad_context = (
        contract_last(grad_attn_all, w_proj).astype(jnp.bfloat16).reshape(total_rows, heads, HEAD)
    )
    prompt_grad_ctx = grad_context[:PROMPT].reshape(blocks, 1, block_rows, heads, HEAD)
    cont_grad_ctx = cont_rows(grad_context)

    def prompt_backward(totals, pieces):
        block_query, block_logs, block_grad = pieces
        grad_query, grad_keys, grad_values = backward_block(
            block_query, prompt_keys, prompt_values, prompt_valid[None], block_logs, block_grad
        )
        return ((totals[0] + grad_keys[0], totals[1] + grad_values[0]), grad_query)

    zero_rows = jnp.zeros((PROMPT, heads, HEAD), jnp.float32)
    prompt_sums, prompt_grad_q = lax.scan(
        prompt_backward, (zero_rows, zero_rows), (prompt_queries, prompt_logs, prompt_grad_ctx)
    )

    def pair_backward(totals, pieces):
        block_query, own_keys, own_values, own_mask, block_logs, block_grad = pieces
        grad_query, grad_keys, grad_values = backward_block(
            block_query,
            pair_keys(prompt_keys, own_keys),
            pair_keys(prompt_values, own_values),
            pair_mask(prompt_valid, own_mask),
            block_logs,
            block_grad,
        )
        new_totals = (
            totals[0] + jnp.sum(grad_keys[:, :PROMPT], axis=0),
            totals[1] + jnp.sum(grad_values[:, :PROMPT], axis=0),
        )
        return (new_totals, (grad_query, grad_keys[:, PROMPT:], grad_values[:, PROMPT:]))

    prompt_sums, pair_grads = lax.scan(
        pair_backward,
        prompt_sums,
        (cont_queries, cont_keys, cont_values, own_valid, pair_logs, cont_grad_ctx),
    )
    grad_query = jnp.concatenate(
        [prompt_grad_q.reshape(PROMPT, width_here), pair_grads[0].reshape(CONT * CLEN, width_here)],
        axis=0,
    ).astype(jnp.bfloat16)
    grad_keys = jnp.concatenate(
        [
            prompt_sums[0].reshape(PROMPT, width_here),
            pair_grads[1].reshape(CONT * CLEN, width_here),
        ],
        axis=0,
    ).astype(jnp.bfloat16)
    grad_values = jnp.concatenate(
        [
            prompt_sums[1].reshape(PROMPT, width_here),
            pair_grads[2].reshape(CONT * CLEN, width_here),
        ],
        axis=0,
    ).astype(jnp.bfloat16)
    grad_proj_rows = jnp.stack([grad_query, grad_keys, grad_values], axis=1)
    grad_b_qv = jnp.stack(
        [
            jnp.sum(grad_query.astype(jnp.float32), axis=0),
            jnp.sum(grad_values.astype(jnp.float32), axis=0),
        ],
        axis=0,
    )
    grad_w_qkv = jnp.einsum(
        "rd,rsf->sdf", attn_input_all, grad_proj_rows, preferred_element_type=jnp.float32
    )
    grad_attn_in = lax.psum_scatter(
        jnp.einsum("rsf,sdf->rd", grad_proj_rows, w_qkv, preferred_element_type=jnp.float32).astype(
            jnp.bfloat16
        ),
        "tensor",
        scatter_dimension=0,
        tiled=True,
    ).astype(jnp.float32)
    input_back, grad_ln1_gain, grad_ln1_bias = norm1_pull(grad_attn_in)
    in_grad = grad_hidden + input_back
    grad_w_qkv, grad_b_qv, grad_w_proj, grad_w_in, grad_b_in, grad_w_out = lax.psum(
        (grad_w_qkv, grad_b_qv, grad_w_proj, grad_w_in, grad_b_in, grad_w_out), "dp"
    )
    grad_b_proj, grad_ln1_gain, grad_ln1_bias, grad_ln2_gain, grad_ln2_bias, grad_b_out = lax.psum(
        (grad_b_proj, grad_ln1_gain, grad_ln1_bias, grad_ln2_gain, grad_ln2_bias, grad_b_out),
        ("dp", "tensor"),
    )
    return (
        layer_out,
        in_grad,
        grad_w_qkv,
        grad_b_qv,
        grad_w_proj,
        grad_b_proj,
        grad_ln1_gain,
        grad_ln1_bias,
        grad_ln2_gain,
        grad_ln2_bias,
        grad_w_in,
        grad_b_in,
        grad_w_out,
        grad_b_out,
    )


def solution(mesh):
    in_specs = (
        P(("dp", "tensor"), None),
        P("dp"),
        P("dp", None),
        P(None, None, "tensor"),
        P(None, "tensor"),
        P("tensor", None),
        P(),
        P(),
        P(),
        P(),
        P(),
        P(None, "tensor"),
        P("tensor"),
        P("tensor", None),
        P(),
        P(("dp", "tensor"), None),
    )
    out_specs = (
        P(("dp", "tensor"), None),
        P(("dp", "tensor"), None),
        P(None, None, "tensor"),
        P(None, "tensor"),
        P("tensor", None),
        P(),
        P(),
        P(),
        P(),
        P(),
        P(None, "tensor"),
        P("tensor"),
        P("tensor", None),
        P(),
    )
    return jax.shard_map(shards, mesh=mesh, in_specs=in_specs, out_specs=out_specs, check_vma=False)
```

profile of v0, /device:TPU:0, one launch (start us, length us, event | category | flops | bytes accessed | tf_op | source)
XLA Modules:
  0.0 934.3 jit_solution(16779138203759255502)
XLA Ops:
  18.1 38.3 %all-gather.5.cloned.1.call-done = bf16[3072,768]{1,0:T(8,128)(2,1)} async-done(((bf16[768,768]{1,0:T(8,128)(2,1)}), bf16[3072,768]{1,0:T(8,128)(2,1)}) %all-gather.5.cloned.1.call-update) | async-done | bytes 4718608 | tf_op jit(solution)/shard_map/all_gather | solution.py:116
  56.4 4.8 fusion.136
  81.9 10.8 %while.60 = (s32[]{:T(128)}, bf16[2,1,512,3,64]{2,4,3,1,0:T(8,128)(2,1)S(1)}, f32[2,1,3,512,1]{3,2,4,1,0:T(4,128)S(1)}, bf16[2,1,512,3,64]{2,4,3,1,0:T(8,128)(2,...) while((s32[]{:T(128)}, ...), condition=%wide.region_5.6_spmd.clone, body=%wide.region_2.5_spmd.clone.sunk | while | flops 421527040 | bytes 20314220 | solution.py:140
  93.8 40.0 %while.61 = (s32[]{:T(128)}, bf16[4,2,256,3,64]{2,4,3,1,0:T(8,128)(2,1)}, f32[4,2,3,256,1]{3,2,1,4,0:T(4,128)}, bf16[1,1024,3,64]{1,3,2,0:T(8,128)(2,1)S(1)}, bf...) while((s32[]{:T(128)}, ...), condition=%wide.region_9.10_spmd.clone, body=%wide.region_6.9_spmd.clone.sunk | while | flops 530843648 | bytes 35660492 | solution.py:151
  147.8 47.3 %reduce-scatter.5.cloned.1.call-done = bf16[768,768]{1,0:T(8,128)(2,1)} async-done(((bf16[3072,768]{1,0:T(8,128)(2,1)}), bf16[768,768]{1,0:T(8,128)(2,1)}) %reduce-scatter.5.cloned.1.call-update) | async-done | bytes 1179664 | tf_op jit(solution)/shard_map/reduce_scatter | solution.py:155
  201.5 36.8 %all-gather.7.cloned.1.call-done = bf16[3072,768]{1,0:T(8,128)(2,1)} async-done(((bf16[768,768]{1,0:T(8,128)(2,1)}), bf16[3072,768]{1,0:T(8,128)(2,1)}) %all-gather.7.cloned.1.call-update) | async-done | bytes 4718608 | tf_op jit(solution)/shard_map/all_gather | solution.py:167
  238.3 11.1 %fusion.137 = f32[3072,768]{1,0:T(8,128)} fusion(bf16[3072,768]{1,0:T(8,128)(2,1)} %all-gather.7.cloned.1.call-done, bf16[768,768]{1,0:T(8,128)(2,1)} %param.35), kind=kOutput, calls=%fused_computation.213 | convolution fusion | flops 3623878656 | bytes 15335424 | tf_op jit(solution)/shard_map/dot_general | solution.py:168
  249.4 27.9 %all-gather.9.cloned.1.call-done = bf16[3072,768]{1,0:T(8,128)(2,1)} async-done(((bf16[768,768]{1,0:T(8,128)(2,1)}), bf16[3072,768]{1,0:T(8,128)(2,1)}) %all-gather.9.cloned.1.call-update) | async-done | bytes 4718608 | tf_op jit(solution)/shard_map/all_gather | solution.py:179
  277.2 28.4 %convert_reduce_fusion = (f32[768]{0:T(1024)}, bf16[3072,768]{1,0:T(8,128)(2,1)S(1)}, f32[3072,768]{1,0:T(8,128)}) fusion(f32[3072,768]{1,0:T(8,128)} %fusion.137, f32[768]{0:T(1024)S(1)} %convert_element_type.154, bf16[3072,768]{1,0:T(8,128)(2,1)} %all-gather.9.cloned.1.call-done, bf16[768,768]{1,0:T(8,128)(2,1)S(1)} %copy-done), kind=kOutput, calls=%fused_computation.127 | convolution fusion | flops 3800825088 | bytes 29497344 | tf_op jit(solution)/shard_map/dot_general | solution.py:81
  307.8 5.6 convolution_convert_fusion
  313.8 10.7 %multiply_convert_fusion.2 = bf16[3072,768]{1,0:T(8,128)(2,1)} fusion(f32[3072,768]{1,0:T(8,128)} %get-tuple-element.594, f32[3072,768]{1,0:T(8,128)} %fusion.137, f32[768]{0:T(1024)S(1)} %convert_element_type.154), kind=kLoop, calls=%fused_computation.129 | loop fusion | flops 9437184 | bytes 23596032 | tf_op jit(solution)/shard_map/convert_element_type | solution.py:172
  324.5 7.9 convolution_convert_fusion.1
  333.1 28.4 %reduce-scatter.9.cloned.1.call-done = bf16[768,768]{1,0:T(8,128)(2,1)} async-done(((bf16[3072,768]{1,0:T(8,128)(2,1)}), bf16[768,768]{1,0:T(8,128)(2,1)}) %reduce-scatter.9.cloned.1.call-update) | async-done | bytes 1179664 | tf_op jit(solution)/shard_map/reduce_scatter | solution.py:187
  364.6 47.1 %reduce-scatter.7.cloned.1.call-done = bf16[768,768]{1,0:T(8,128)(2,1)} async-done(((bf16[3072,768]{1,0:T(8,128)(2,1)}), bf16[768,768]{1,0:T(8,128)(2,1)}) %reduce-scatter.7.cloned.1.call-update) | async-done | bytes 1179664 | tf_op jit(solution)/shard_map/reduce_scatter | solution.py:173
  419.4 37.1 %all-gather.11.cloned.1.call-done = bf16[3072,768]{1,0:T(8,128)(2,1)} async-done(((bf16[768,768]{1,0:T(8,128)(2,1)}), bf16[3072,768]{1,0:T(8,128)(2,1)}) %all-gather.11.cloned.1.call-update) | async-done | bytes 4718608 | tf_op jit(solution)/shard_map/all_gather | solution.py:199
  462.5 20.6 %while.63 = (s32[]{:T(128)}, f32[1024,3,64]{0,2,1:T(8,128)S(1)}, f32[1024,3,64]{0,2,1:T(8,128)}, bf16[2,1,512,3,64]{2,4,3,1,0:T(8,128)(2,1)S(1)}, bf16[2,1,512,3...) while((s32[]{:T(128)}, f32[1024,3,64]{0,2,1:T(8,128)S(1)}, ...), condition=%wide.region_19.20_spmd.clone, body=%wide.region_17.19_spmd.clone.sunk | while | flops 1031306752 | bytes 52742304 | solution.py:217
  487.3 122.6 %while.62 = (s32[]{:T(128)}, f32[1024,3,64]{0,2,1:T(8,128)S(1)}, f32[1024,3,64]{0,2,1:T(8,128)}, bf16[4,2,256,3,64]{2,4,3,1,0:T(8,128)(2,1)}, bf16[4,2,256,3,64]...) while((s32[]{:T(128)}, f32[1024,3,64]{0,2,1:T(8,128)S(1)}, ...), condition=%wide.region_24.25_spmd.clone, body=%wide.region_20.24_spmd.clone.sunk | while | flops 1283262464 | bytes 120956472 | solution.py:237
  494.2 5.9 multiply_reduce_fusion.5
  500.1 6.3 multiply_convert_fusion.5
  524.7 5.9 multiply_reduce_fusion.5
  530.7 6.3 multiply_convert_fusion.5
  555.3 5.9 multiply_reduce_fusion.5
  561.2 6.3 multiply_convert_fusion.5
  567.5 4.3 fusion.211
  585.8 5.9 multiply_reduce_fusion.5
  591.8 6.3 multiply_convert_fusion.5
  622.4 7.9 bitcast_convert_fusion
  630.7 9.2 fusion.139
  639.9 9.7 %fusion.140 = f32[768,768]{1,0:T(8,128)} fusion(bf16[3072,768]{1,0:T(8,128)(2,1)} %multiply_convert_fusion.2, bf16[3072,768]{1,0:T(8,128)(2,1)} %all-gather.9.cloned.1.call-done), kind=kOutput, calls=%fused_computation.216 | convolution fusion | flops 3623878656 | bytes 11796480 | tf_op jit(solution)/shard_map/rf,rd->fd/dot_general | solution.py:182
  663.4 22.7 %all-reduce.1 = (f32[2,192]{1,0:T(2,128)}, f32[768]{0:T(1024)}) all-reduce(f32[2,192]{1,0:T(2,128)} %pad_maximum_fusion.3, f32[768]{0:T(1024)} %get-tuple-element.592), channel_id=1, replica_groups=mesh['dp'=8,'tensor'=4] {'dp'}, use_global_device_ids=true, to_apply=%region_31.32 | all-reduce | flops 1152 | bytes 9216 | tf_op jit(solution)/shard_map/psum | solution.py:281
  696.0 41.2 %all-reduce = (f32[768]{0:T(1024)}, f32[768]{0:T(1024)}, f32[768]{0:T(1024)}, f32[768]{0:T(1024)}, f32[768]{0:T(1024)}, /*index=5*/f32[768]{0:T(1024)}) all-reduce(f32[768]{0:T(1024)} %get-tuple-element.590, f32[768]{0:T(1024)} %get-tuple-element.489, ...), channel_id=1, replica_groups=mesh['dp'=8,'tensor'=4] {'dp','tensor'}, use_global_device_ids=true, to_apply=%region_34.35 | all-reduce | flops 4608 | bytes 36864 | tf_op jit(solution)/shard_map/psum | solution.py:284
  737.2 183.5 %all-reduce.5.cloned.1.call-done = (f32[3,768,192]{1,2,0:T(8,128)}, f32[192,768]{1,0:T(8,128)}, f32[768,768]{1,0:T(8,128)}, f32[768,768]{1,0:T(8,128)}) async-done(((f32[3,768,192]{1,2,0:T(8,128)}, f32[192,768]{1,0:T(8,128)}, f32[768,768]{1,0:T(8,128)}, f32[768,768]{1,0:T(8,128)}), (f32[3,768,192]{1,2,0:T(8,128)}, f32[192,768]{1,0:T(8,128)}, f32[768,768]{1,0:T(8,128)}, ...) | async-done | bytes 7077904 | tf_op jit(solution)/shard_map/psum | solution.py:281
  (475 shorter events, 258.6 us)
Async XLA Ops:
  7.2 270.1 %copy-start = (bf16[768,768]{1,0:T(8,128)(2,1)S(1)}, bf16[768,768]{1,0:T(8,128)(2,1)}, u32[]{:S(2)}) copy-start(bf16[768,768]{1,0:T(8,128)(2,1)} %param.37) | copy-start | bytes 3538948
  7.2 9.5 %copy-start.60 = (s32[1,8]{1,0:T(1,128)S(1)}, s32[1,8]{1,0:T(1,128)}, u32[]{:S(2)}) copy-start(s32[1,8]{1,0:T(1,128)} %param.26) | copy-start | bytes 100
  7.2 10.2 %copy-start.52 = (bf16[2,192]{1,0:T(2,128)(2,1)S(1)}, bf16[2,192]{1,0:T(2,128)(2,1)}, u32[]{:S(2)}) copy-start(bf16[2,192]{1,0:T(2,128)(2,1)} %param.28) | copy-start | bytes 2308
  7.2 49.2 %copy-start.59 = (bf16[3,768,192]{1,2,0:T(8,128)(2,1)S(1)}, bf16[3,768,192]{1,2,0:T(8,128)(2,1)}, u32[]{:S(2)}) copy-start(bf16[3,768,192]{1,2,0:T(8,128)(2,1)} %param.27) | copy-start | bytes 2654212
  7.2 49.1 %all-gather.5.cloned.1.call-start = ((), (), s32[]{:S(2)}) async-start(), calls=%async_computation.4 | async-start | bytes 5898240 | tf_op jit(solution)/shard_map/all_gather | solution.py:116
  16.1 179.1 %reduce-scatter.5.cloned.1.call-start = ((), (), s32[]{:S(2)}) async-start(), calls=%async_computation.5 | async-start | bytes 5898240 | tf_op jit(solution)/shard_map/reduce_scatter | solution.py:155
  65.1 11.0 %copy-start.32 = (bf16[1024,192]{0,1:T(8,128)(2,1)S(1)}, bf16[1024,192]{0,1:T(8,128)(2,1)}, u32[]{:S(2)}) copy-start(bf16[1024,192]{0,1:T(8,128)(2,1)} %slice.84) | copy-start | bytes 1179652
  133.8 9.7 %copy-start.40 = (bf16[192,768]{1,0:T(8,128)(2,1)S(1)}, bf16[192,768]{1,0:T(8,128)(2,1)}, u32[]{:S(2)}) copy-start(bf16[192,768]{1,0:T(8,128)(2,1)} %param.29) | copy-start | bytes 884740
  147.1 48.0 %copy-start.5 = (bf16[768,768]{1,0:T(8,128)(2,1)S(1)}, bf16[768,768]{1,0:T(8,128)(2,1)}, u32[]{:S(2)}) copy-start(bf16[768,768]{1,0:T(8,128)(2,1)} %param.24) | copy-start | bytes 3538948
  147.2 91.1 %all-gather.7.cloned.1.call-start = ((), (), s32[]{:S(2)}) async-start(), calls=%async_computation.6 | async-start | bytes 5898240 | tf_op jit(solution)/shard_map/all_gather | solution.py:167
  200.6 76.6 %all-gather.9.cloned.1.call-start = ((), (), s32[]{:S(2)}) async-start(), calls=%async_computation.8 | async-start | bytes 5898240 | tf_op jit(solution)/shard_map/all_gather | solution.py:179
  201.2 160.3 %reduce-scatter.9.cloned.1.call-start = ((), (), s32[]{:S(2)}) async-start(), calls=%async_computation.9 | async-start | bytes 5898240 | tf_op jit(solution)/shard_map/reduce_scatter | solution.py:187
  277.2 30.6 %copy-start.58 = (bf16[768,768]{1,0:T(8,128)(2,1)S(1)}, bf16[768,768]{1,0:T(8,128)(2,1)}, u32[]{:S(2)}) copy-start(bf16[768,768]{1,0:T(8,128)(2,1)} %param.35) | copy-start | bytes 3538948
  313.5 98.3 %reduce-scatter.7.cloned.1.call-start = ((), (), s32[]{:S(2)}) async-start(), calls=%async_computation.7 | async-start | bytes 5898240 | tf_op jit(solution)/shard_map/reduce_scatter | solution.py:173
  332.4 29.1 %copy-start.15 = (bf16[768,768]{1,0:T(8,128)(2,1)S(1)}, bf16[768,768]{1,0:T(8,128)(2,1)}, u32[]{:S(2)}) copy-start(bf16[768,768]{1,0:T(8,128)(2,1)} %reduce-scatter.5.cloned.1.call-done) | copy-start | bytes 3538948
  332.5 124.0 %all-gather.11.cloned.1.call-start = ((), (), s32[]{:S(2)}) async-start(), calls=%async_computation.10 | async-start | bytes 5898240 | tf_op jit(solution)/shard_map/all_gather | solution.py:199
  415.4 45.1 %copy-start.49 = (f32[768]{0:T(1024)}, f32[768]{0:T(1024)S(1)}, u32[]{:S(2)}) copy-start(f32[768]{0:T(1024)S(1)} %negate_multiply_fusion.2) | copy-start | bytes 9220
  418.9 267.3 %reduce-scatter.11.cloned.1.call-start = ((), (), s32[]{:S(2)}) async-start(), calls=%async_computation.11 | async-start | bytes 5898240 | tf_op jit(solution)/shard_map/reduce_scatter | solution.py:271
  611.9 9.2 copy-start.25
  613.1 38.4 %copy-start.34 = (bf16[1024,3,64]{0,2,1:T(8,128)(2,1)}, bf16[1024,3,64]{0,2,1:T(8,128)(2,1)S(1)}, u32[]{:S(2)}) copy-start(bf16[1024,3,64]{0,2,1:T(8,128)(2,1)S(1)} %convert.50) | copy-start | bytes 1179652
  630.3 290.3 %all-reduce.5.cloned.1.call-start = ((), (), s32[]{:S(2)}) async-start(), calls=%async_computation.12 | async-start | bytes 14155776 | tf_op jit(solution)/shard_map/psum | solution.py:281
  630.6 18.9 %slice-start = ((s8[4718592]{0:T(1024)(128)(4,1)}), s8[4194304]{0:T(1024)(128)(4,1)S(1)}, s32[]{:S(2)}) async-start(s8[4718592]{0:T(1024)(128)(4,1)} %bitcast.321), calls=%async_computation.13 | async-start | bytes 8388608
  630.6 20.9 %slice-start.2 = ((s8[4718592]{0:T(1024)(128)(4,1)}), s8[4194304]{0:T(1024)(128)(4,1)S(1)}, s32[]{:S(2)}) async-start(s8[4718592]{0:T(1024)(128)(4,1)} %bitcast.336), calls=%async_computation.15 | async-start | bytes 8388608
  639.9 9.7 %copy-start.21 = (bf16[3072,192]{0,1:T(8,128)(2,1)S(1)}, bf16[3072,192]{0,1:T(8,128)(2,1)}, u32[]{:S(2)}) copy-start(bf16[3072,192]{0,1:T(8,128)(2,1)} %copy-done.20) | copy-start | bytes 3538948
  639.9 9.7 %slice-start.1 = ((s8[4718592]{0:T(1024)(128)(4,1)}), s8[524288]{0:T(1024)(128)(4,1)S(1)}, s32[]{:S(2)}) async-start(s8[4718592]{0:T(1024)(128)(4,1)} %bitcast.321), calls=%async_computation.14 | async-start | bytes 1048576
  639.9 11.7 %slice-start.3 = ((s8[4718592]{0:T(1024)(128)(4,1)}), s8[524288]{0:T(1024)(128)(4,1)S(1)}, s32[]{:S(2)}) async-start(s8[4718592]{0:T(1024)(128)(4,1)} %bitcast.336), calls=%async_computation.16 | async-start | bytes 1048576
  655.8 30.4 %copy-start.6 = (bf16[768,768]{1,0:T(8,128)(2,1)S(1)}, bf16[768,768]{1,0:T(8,128)(2,1)}, u32[]{:S(2)}) copy-start(bf16[768,768]{1,0:T(8,128)(2,1)} %param.24) | copy-start | bytes 3538948
  655.8 30.4 %copy-start.42 = (f32[768]{0:T(1024)S(1)}, f32[768]{0:T(1024)}, u32[]{:S(2)}) copy-start(f32[768]{0:T(1024)} %copy-done.41) | copy-start | bytes 9220
  655.8 30.4 %copy-start.44 = (f32[768]{0:T(1024)S(1)}, f32[768]{0:T(1024)}, u32[]{:S(2)}) copy-start(f32[768]{0:T(1024)} %copy-done.43) | copy-start | bytes 9220
  657.3 32.4 %copy-start.48 = (f32[768]{0:T(1024)S(1)}, f32[768]{0:T(1024)}, u32[]{:S(2)}) copy-start(f32[768]{0:T(1024)} %copy-done.47) | copy-start | bytes 9220
  658.8 34.2 %copy-start.19 = (f32[768,768]{1,0:T(8,128)S(1)}, f32[768,768]{1,0:T(8,128)}, u32[]{:S(2)}) copy-start(f32[768,768]{1,0:T(8,128)} %copy-done.18) | copy-start | bytes 7077892
  658.8 34.2 %copy-start.50 = (f32[768]{0:T(1024)S(1)}, f32[768]{0:T(1024)}, u32[]{:S(2)}) copy-start(f32[768]{0:T(1024)} %copy-done.49) | copy-start | bytes 9220
  (85 other events, 260.3 us)
Sparse Core Ops, SparseCore 0:
  16.2 40.1 all-gather.4
  147.3 47.8 reduce-scatter.4
  200.7 37.4 all-gather.6
  239.7 37.4 all-gather.8
  313.6 47.8 reduce-scatter.8
  363.9 47.8 reduce-scatter.6
  419.0 37.4 all-gather.10
  630.5 47.8 reduce-scatter.10
  683.9 236.7 all-reduce.4
where the time goes:
time: 945 us; the launch traced here: 934 us
  waiting for transfers between devices  447 us (47%)
  matrix products  197 us (21%)
  other arithmetic  110 us (12%)
  local copies, waits for them, and re-layouts  97.5 us (10%)
  blocking collectives  64 us (7%)
  between operations  15 us (2%)
    psum x1, waiting for transfers between devices, shards(): lax.psum((grad_w_qkv, grad_b_qv, grad_w_proj, grad_w_in, grad_b_in, grad_...  183 us
    reduce_scatter x1, waiting for transfers between devices, shards(): lax.psum_scatter(jnp.dot(context, w_proj, preferred_element_type=jnp.floa...  47.3 us
    reduce_scatter x1, waiting for transfers between devices, shards(): lax.psum_scatter(jnp.dot(gelu_rows, w_out, preferred_element_type=jnp.flo...  47.1 us
    psum x1, blocking collectives, shards(): lax.psum((grad_b_proj, grad_ln1_gain, grad_ln1_bias, grad_ln2_gain, grad_...  41.2 us
    all_gather x1, waiting for transfers between devices, shards(): attn_input_all = lax.all_gather(attn_input, 'tensor', axis=0, tiled=True)  38.3 us
    dot_general x3, matrix products, contract_last(): lax.dot_general(left, right, (((1,), (1,)), ((), ())), preferred_element_...  38 us
    dot_general x12, matrix products, block_scores(): jnp.einsum('bqhe,bkhe->bhqk', queries, key_rows, preferred_element_type=j...  37.2 us
    all_gather x1, waiting for transfers between devices, shards(): grad_attn_all = lax.all_gather(grad_attn, 'tensor', axis=0, tiled=True)  37.1 us
  transfers between devices with their start and end apart: 9, of which 8 were waited for; matrix products, arithmetic and copies ran while one was open for 8% of the time, Pallas kernels for 0%

commit v1 on v0

v1 whole, which is shorter than its diff:
```python
import jax
import jax.numpy as jnp
from jax import lax
from jax.experimental import pallas as pl
from jax.experimental.pallas import tpu as pltpu
from jax.sharding import PartitionSpec as P

HEAD = 64
PROMPT = 1024
CONT = 8
CLEN = 256
PIECES = 4

EPS = 1e-06
MASKED = -1000000000.0
BF = jnp.bfloat16
F32 = jnp.float32


def nt(a, b):
    return lax.dot_general(a, b, (((1,), (1,)), ((), ())), preferred_element_type=F32)


def nn(a, b):
    return lax.dot_general(a, b, (((1,), (0,)), ((), ())), preferred_element_type=F32)


def tn(a, b):
    return lax.dot_general(a, b, (((0,), (0,)), ((), ())), preferred_element_type=F32)


def own_lanes(rows, h):
    lane = lax.broadcasted_iota(jnp.int32, (rows, 128), 1)
    return ((lane < 64) if h == 0 else (lane >= 64)), lane - (64 if h == 0 else 0)


def key_aug(k, h, length, base):
    rows = k.shape[0]
    own, extra = own_lanes(rows, h)
    row = lax.broadcasted_iota(jnp.int32, (rows, 128), 0) + base
    bias = jnp.where(jnp.logical_and(extra == 0, row >= length), MASKED, 0.0)
    return jnp.where(own, k.astype(F32), bias).astype(BF)


def query_aug(q, h):
    own, extra = own_lanes(q.shape[0], h)
    return jnp.where(own, q.astype(F32) * 0.125, jnp.where(extra == 0, 1.0, 0.0)).astype(BF)


def value_aug(v, h):
    own, extra = own_lanes(v.shape[0], h)
    ones = jnp.where(jnp.logical_and(extra >= 0, extra < 3), 1.0, 0.0)
    return jnp.where(own, v.astype(F32), ones).astype(BF)


def transposed(v):
    return v.astype(F32).T


def attn_fwd_kernel(lens, q_ref, kp_ref, vp_ref, ko_ref, vo_ref, ctx_ref, lse_ref, kph, vpt):
    blocks = q_ref.shape[0] // CLEN
    prompt = kp_ref.shape[0]
    vt = transposed(vp_ref[...])
    for h in range(2):
        kph[h] = key_aug(kp_ref[...], h, lens[0], 0)
        vpt[h] = jnp.concatenate([vt[64 * h : 64 * h + 64].astype(BF), jnp.ones((16, prompt), BF)], axis=0)

    def block(b, _):
        rows = pl.ds(pl.multiple_of(b * CLEN, CLEN), CLEN)
        q = q_ref[rows, :]
        ko = ko_ref[rows, :]
        vot = transposed(vo_ref[rows, :])
        outs, logs = [], []
        for h in range(2):
            qh = query_aug(q, h)
            vh = jnp.concatenate([vot[64 * h : 64 * h + 64].astype(BF), jnp.ones((16, CLEN), BF)], axis=0)
            sp = nt(kph[h], qh)
            so = nt(key_aug(ko, h, lens[1 + b], 0), qh)
            top = jnp.maximum(jnp.max(sp, axis=0, keepdims=True), jnp.max(so, axis=0, keepdims=True))
            pp = jnp.exp(sp - top).astype(BF)
            po = jnp.exp(so - top).astype(BF)
            ot = nn(vpt[h], pp) + nn(vh, po)
            total = ot[64:65]
            outs.append(ot[:64] * (1.0 / total))
            logs.append(top + jnp.log(total))
        ctx_ref[rows, :] = jnp.concatenate(outs, axis=0).T.astype(BF)
        lse_ref[0, b] = jnp.concatenate(logs + [jnp.zeros((6, CLEN), F32)], axis=0)
        return 0

    lax.fori_loop(0, blocks, block, 0)


def attn_bwd_kernel(lens, q_ref, kp_ref, vp_ref, ko_ref, vo_ref, do_ref, ctx_ref, lse_ref,
                    dq_ref, dkp_ref, dvp_ref, dko_ref, dvo_ref, qh_s, doh_s, dqt):
    rows_all = q_ref.shape[0]
    blocks = rows_all // CLEN
    chunks = kp_ref.shape[0] // CLEN
    prod = do_ref[...].astype(F32) * ctx_ref[...].astype(F32)
    for h in range(2):
        own, extra = own_lanes(rows_all, h)
        qh_s[h] = query_aug(q_ref[...], h)
        d = -jnp.sum(jnp.where(own, prod, 0.0), axis=1, keepdims=True)
        hi = d.astype(BF).astype(F32)
        mid = (d - hi).astype(BF).astype(F32)
        low = d - hi - mid
        aug = jnp.where(extra == 0, hi, jnp.where(extra == 1, mid, jnp.where(extra == 2, low, 0.0)))
        doh_s[h] = jnp.where(own, do_ref[...].astype(F32), aug).astype(BF)
    first = lax.broadcasted_iota(jnp.int32, (CLEN, 128), 1) < 64

    def own_block(b, _):
        rows = pl.ds(pl.multiple_of(b * CLEN, CLEN), CLEN)
        q = q_ref[rows, :]
        k = ko_ref[rows, :]
        v = vo_ref[rows, :]
        do = do_ref[rows, :]
        kt = transposed(k).astype(BF)
        dks, dvs, dqs = [], [], []
        for h in range(2):
            s = nt(key_aug(k, h, lens[1 + b], 0), qh_s[h, rows, :])
            p = jnp.exp(s - lse_ref[0, b, h : h + 1, :])
            dp = nt(value_aug(v, h), doh_s[h, rows, :])
            ds = (p * dp).astype(BF)
            dvs.append(nn(p.astype(BF), do))
            dks.append(nn(ds, q))
            dqs.append(nn(kt[64 * h : 64 * h + 64], ds))
        dvo_ref[rows, :] = jnp.where(first, dvs[0], dvs[1]).astype(BF)
        dko_ref[rows, :] = (jnp.where(first, dks[0], dks[1]) * 0.125).astype(BF)
        dqt[b] = jnp.concatenate(dqs, axis=0)
        return 0

    lax.fori_loop(0, blocks, own_block, 0)

    def chunk(c, _):
        rows = pl.ds(pl.multiple_of(c * CLEN, CLEN), CLEN)
        k = kp_ref[rows, :]
        v = vp_ref[rows, :]
        kt = transposed(k).astype(BF)
        dks, dvs = [], []
        for h in range(2):
            kh = key_aug(k, h, lens[0], c * CLEN)
            vh = value_aug(v, h)
            dk = dv = None
            for b in range(blocks):
                rb = pl.ds(b * CLEN, CLEN)
                s = nt(kh, qh_s[h, rb, :])
                p = jnp.exp(s - lse_ref[0, b, h : h + 1, :])
                dp = nt(vh, doh_s[h, rb, :])
                ds = (p * dp).astype(BF)
                dv_b = nn(p.astype(BF), do_ref[rb, :])
                dk_b = nn(ds, q_ref[rb, :])
                dv = dv_b if b == 0 else dv + dv_b
                dk = dk_b if b == 0 else dk + dk_b
                dqt[b, 64 * h : 64 * h + 64] += nn(kt[64 * h : 64 * h + 64], ds)
            dvs.append(dv)
            dks.append(dk)
        dvp_ref[rows, :] = jnp.where(first, dvs[0], dvs[1]).astype(BF)
        dkp_ref[rows, :] = (jnp.where(first, dks[0], dks[1]) * 0.125).astype(BF)
        return 0

    lax.fori_loop(0, chunks, chunk, 0)
    for b in range(blocks):
        dq_ref[b * CLEN : (b + 1) * CLEN, :] = (dqt[b].T * 0.125).astype(BF)


def attn_specs(rows, prompt, blocks):
    def col(n):
        return pl.BlockSpec((n, 128), lambda i, l: (0, i))

    logs = pl.BlockSpec((1, blocks, 8, CLEN), lambda i, l: (i, 0, 0, 0))
    return col(rows), col(prompt), logs


def attn_fwd(lens, q, kp, vp, ko, vo):
    rows, width = q.shape
    prompt = kp.shape[0]
    blocks = rows // CLEN
    pairs = width // 128
    r, p, logs = attn_specs(rows, prompt, blocks)
    cells = rows * (prompt + CLEN) * pairs * 2
    return pl.pallas_call(
        attn_fwd_kernel,
        out_shape=(
            jax.ShapeDtypeStruct((rows, width), BF),
            jax.ShapeDtypeStruct((pairs, blocks, 8, CLEN), F32),
        ),
        grid_spec=pltpu.PrefetchScalarGridSpec(
            num_scalar_prefetch=1,
            grid=(pairs,),
            in_specs=[r, p, p, r, r],
            out_specs=[r, logs],
            scratch_shapes=[pltpu.VMEM((2, prompt, 128), BF), pltpu.VMEM((2, 80, prompt), BF)],
        ),
        compiler_params=pltpu.CompilerParams(vmem_limit_bytes=40 << 20),
        cost_estimate=pl.CostEstimate(
            flops=cells * 256 * 4, transcendentals=cells, bytes_accessed=2 * width * (4 * rows + 2 * prompt)
        ),
        name="attn_fwd",
    )(lens, q, kp, vp, ko, vo)


def attn_bwd(lens, q, kp, vp, ko, vo, do, ctx, lse):
    rows, width = q.shape
    prompt = kp.shape[0]
    blocks = rows // CLEN
    pairs = width // 128
    r, p, logs = attn_specs(rows, prompt, blocks)
    cells = rows * (prompt + CLEN) * pairs * 2

    def shape(n):
        return jax.ShapeDtypeStruct((n, width), BF)

    return pl.pallas_call(
        attn_bwd_kernel,
        out_shape=(shape(rows), shape(prompt), shape(prompt), shape(rows), shape(rows)),
        grid_spec=pltpu.PrefetchScalarGridSpec(
            num_scalar_prefetch=1,
            grid=(pairs,),
            in_specs=[r, p, p, r, r, r, r, logs],
            out_specs=[r, p, p, r, r],
            scratch_shapes=[
                pltpu.VMEM((2, rows, 128), BF),
                pltpu.VMEM((2, rows, 128), BF),
                pltpu.VMEM((blocks, 128, CLEN), F32),
            ],
        ),
        compiler_params=pltpu.CompilerParams(vmem_limit_bytes=40 << 20),
        cost_estimate=pl.CostEstimate(
            flops=cells * 256 * 10, transcendentals=cells, bytes_accessed=2 * width * (8 * rows + 4 * prompt)
        ),
        name="attn_bwd",
    )(lens, q, kp, vp, ko, vo, do, ctx, lse)


def swap(v, axis, bit):
    return lax.ppermute(v, axis, [(i, i ^ bit) for i in range(lax.axis_size(axis))])


def gather_pieces(own):
    side = swap(own, "tensor", 1)
    across = swap(own, "tensor", 2)
    return [own, side, across, swap(across, "tensor", 1)]


def tensor_sum(pieces):
    g0, g1, g2, g3 = pieces
    r1 = swap(g1.astype(BF), "tensor", 1)
    r3 = swap(g3.astype(BF), "tensor", 1)
    r2 = swap((g2 + r3.astype(F32)).astype(BF), "tensor", 2)
    return g0 + r1.astype(F32) + r2.astype(F32)


def dp_sum(total):
    size = lax.axis_size("dp")
    me = lax.axis_index("dp")
    bits = [b for b in range(size.bit_length()) if (1 << b) < size]
    value = total
    for b in bits:
        half = value.shape[0] // 2
        upper = (me >> b) & 1
        low, high = value[:half], value[half:]
        away = jnp.where(upper == 0, high, low).astype(BF)
        keep = jnp.where(upper == 0, low, high)
        value = keep + swap(away, "dp", 1 << b).astype(F32)
    value = value.astype(BF)
    for b in reversed(bits):
        upper = (me >> b) & 1
        other = swap(value, "dp", 1 << b)
        value = jnp.concatenate([jnp.where(upper == 0, value, other), jnp.where(upper == 0, other, value)], axis=0)
    return value.astype(F32)


def normalize(values):
    centred = values - jnp.mean(values, axis=-1, keepdims=True)
    scale = lax.rsqrt(jnp.mean(centred * centred, axis=-1, keepdims=True) + EPS)
    return centred * scale, scale


def norm_back(grad, normal, scale, gain):
    e = grad * gain
    back = scale * (e - jnp.mean(e, axis=-1, keepdims=True) - normal * jnp.mean(e * normal, axis=-1, keepdims=True))
    return back, jnp.sum(grad * normal, axis=0), jnp.sum(grad, axis=0)


def shards(layer_in, prompt_len, cont_len, w_qkv, b_qv, w_proj, b_proj, ln1_gain, ln1_bias,
           ln2_gain, ln2_bias, w_in, b_in, w_out, b_out, out_grad):
    rows, width = layer_in.shape
    blocks = rows // CLEN
    t = lax.axis_index("tensor")
    odd = (t & 1) == 1
    half_prompt = PROMPT // 2
    g1, c1, g2, c2 = (v.astype(F32) for v in (ln1_gain, ln1_bias, ln2_gain, ln2_bias))

    beside = swap(layer_in, "tensor", 1)
    even_rows = jnp.where(odd, beside, layer_in)
    odd_rows = jnp.where(odd, layer_in, beside)
    here = jnp.concatenate([even_rows, odd_rows[: PROMPT - rows]], axis=0)
    part = jnp.where(odd, here[half_prompt:], here[:half_prompt])
    came = lax.ppermute(part, "tensor", [(0, 2), (1, 3)])
    came_beside = swap(came, "tensor", 1)
    there = jnp.concatenate([jnp.where(odd, came_beside, came), jnp.where(odd, came, came_beside)], axis=0)
    prompt_rows = jnp.where(t < 2, here, there)

    bias_rows = jnp.stack([b_qv[0], jnp.zeros_like(b_qv[0]), b_qv[1]], axis=0)[:, None, :]
    qkv_pack = jnp.concatenate([w_qkv, jnp.pad(bias_rows, ((0, 0), (0, 15), (0, 0)))], axis=1)
    qkv_pieces = gather_pieces(qkv_pack)
    proj_pieces = gather_pieces(w_proj)
    in_pieces = gather_pieces(jnp.concatenate([w_in, jnp.pad(b_in[None], ((0, 15), (0, 0)))], axis=0))
    out_pieces = gather_pieces(w_out)

    rows_in = layer_in.astype(F32)
    normal1, scale1 = normalize(rows_in)
    attn_input = (normal1 * g1 + c1).astype(BF)
    normal_p, _ = normalize(prompt_rows.astype(F32))
    prompt_input = (normal_p * g1 + c1).astype(BF)

    group = t * blocks + jnp.arange(blocks)
    conts = group - PROMPT // CLEN
    own_len = jnp.where(conts >= 0, cont_len[0][jnp.clip(conts, 0, CONT - 1)], 0)
    lens = jnp.concatenate([prompt_len, own_len]).astype(jnp.int32)

    units = []
    for u in range(2):
        pack = jnp.concatenate([qkv_pieces[2 * u], qkv_pieces[2 * u + 1]], axis=2)
        w = pack[:, :width]
        bias = pack[:, width].astype(F32)
        q = (nn(attn_input, w[0]) + bias[0]).astype(BF)
        ko = nn(attn_input, w[1]).astype(BF)
        vo = (nn(attn_input, w[2]) + bias[2]).astype(BF)
        kp = nn(prompt_input, w[1]).astype(BF)
        vp = (nn(prompt_input, w[2]) + bias[2]).astype(BF)
        ctx, lse = attn_fwd(lens, q, kp, vp, ko, vo)
        units.append((w, q, kp, vp, ko, vo, ctx, lse))

    proj_units = [jnp.concatenate(proj_pieces[2 * u : 2 * u + 2], axis=0) for u in range(2)]
    attn_out = nn(units[0][6], proj_units[0]) + nn(units[1][6], proj_units[1]) + b_proj.astype(F32)
    hidden = rows_in + attn_out
    normal2, scale2 = normalize(hidden)
    mlp_input = (normal2 * g2 + c2).astype(BF)

    branch = 0.0
    grad_mlp_in = 0.0
    grad_in_pieces, grad_out_pieces, grad_b_in_pieces = [], [], []
    for r in range(PIECES):
        w1 = in_pieces[r][:width]
        pre = nn(mlp_input, w1) + in_pieces[r][width].astype(F32)
        cdf = 0.5 * (1.0 + lax.erf(pre * (0.5**0.5)))
        pdf = jnp.exp(-0.5 * pre * pre) * 0.3989422804014327
        gelu = (pre * cdf).astype(BF)
        branch = branch + nn(gelu, out_pieces[r])
        grad_pre = (nt(out_grad, out_pieces[r]) * (cdf + pre * pdf)).astype(BF)
        grad_out_pieces.append(tn(gelu, out_grad))
        grad_in_pieces.append(tn(mlp_input, grad_pre))
        grad_b_in_pieces.append(jnp.sum(grad_pre.astype(F32), axis=0))
        grad_mlp_in = grad_mlp_in + nt(grad_pre, w1)
    layer_out = (hidden + (branch + b_out.astype(F32))).astype(BF)

    grad_w_out = dp_sum(tensor_sum(grad_out_pieces))
    grad_w_in = dp_sum(tensor_sum(grad_in_pieces))

    back2, sum_g2, sum_c2 = norm_back(grad_mlp_in, normal2, scale2, g2)
    dy = out_grad.astype(F32)
    grad_hidden = dy + back2
    grad_attn = grad_hidden.astype(BF)
    sum_b_proj = jnp.sum(grad_attn.astype(F32), axis=0)
    sum_b_out = jnp.sum(dy, axis=0)

    grad_own_in = 0.0
    grad_prompt_in = 0.0
    grad_qkv_pieces, grad_proj_pieces, sum_qv_pieces = [None] * 4, [None] * 4, [None] * 4
    both_input = jnp.concatenate([attn_input, prompt_input], axis=0)
    for u in (1, 0):
        w, q, kp, vp, ko, vo, ctx, lse = units[u]
        grad_proj = tn(ctx, grad_attn)
        grad_ctx = nt(grad_attn, proj_units[u]).astype(BF)
        dq, dkp, dvp, dko, dvo = attn_bwd(lens, q, kp, vp, ko, vo, grad_ctx, ctx, lse)
        grad_own_in = grad_own_in + nt(dq, w[0]) + nt(dko, w[1]) + nt(dvo, w[2])
        grad_prompt_in = grad_prompt_in + nt(dkp, w[1]) + nt(dvp, w[2])
        gq = tn(attn_input, dq)
        gk = tn(both_input, jnp.concatenate([dko, dkp], axis=0))
        gv = tn(both_input, jnp.concatenate([dvo, dvp], axis=0))
        sum_q = jnp.sum(dq.astype(F32), axis=0)
        sum_v = jnp.sum(dvo.astype(F32), axis=0) + jnp.sum(dvp.astype(F32), axis=0)
        part_width = gq.shape[1] // 2
        for k in range(2):
            cols = slice(k * part_width, (k + 1) * part_width)
            grad_qkv_pieces[2 * u + k] = jnp.concatenate([gq[:, cols], gk[:, cols], gv[:, cols]], axis=0)
            grad_proj_pieces[2 * u + k] = grad_proj[cols]
            sum_qv_pieces[2 * u + k] = jnp.concatenate([sum_q[cols], sum_v[cols]])
    grad_w_proj = dp_sum(tensor_sum(grad_proj_pieces))
    grad_w_qkv = dp_sum(tensor_sum(grad_qkv_pieces)).reshape((3, width, -1))

    share = grad_prompt_in.astype(BF)
    low, high = share[:half_prompt], share[half_prompt:]
    mine = jnp.where(odd, high, low).astype(F32) + swap(jnp.where(odd, low, high), "tensor", 1).astype(F32)
    mine = mine + lax.ppermute(mine.astype(BF), "tensor", [(2, 0), (3, 1)]).astype(F32)
    spare = rows - half_prompt
    tail = lax.ppermute(mine[:spare].astype(BF), "tensor", [(1, 0)]).astype(F32)
    first_rows = jnp.concatenate([mine, tail], axis=0)
    next_rows = jnp.concatenate([mine[spare:], jnp.zeros((rows - half_prompt + spare, width), F32)], axis=0)
    extra = jnp.where(t == 0, first_rows, jnp.where(t == 1, next_rows, 0.0))
    back1, sum_g1, sum_c1 = norm_back(grad_own_in + extra, normal1, scale1, g1)
    in_grad = grad_hidden + back1

    def ordered(pieces):
        pieces = [jnp.where(odd, pieces[r ^ 1], pieces[r]) for r in range(PIECES)]
        return [jnp.where(t >= 2, pieces[r ^ 2], pieces[r]) for r in range(PIECES)]

    small = jnp.concatenate(
        [sum_b_proj, sum_g1, sum_c1, sum_g2, sum_c2, sum_b_out] + ordered(grad_b_in_pieces) + ordered(sum_qv_pieces)
    )
    small = lax.psum(small, ("dp", "tensor"))
    sums = [small[k * width : (k + 1) * width] for k in range(6)]
    at = 6 * width
    hid = w_in.shape[1]
    grad_b_in = lax.dynamic_slice(small, (at + t * hid,), (hid,))
    qv = 2 * w_qkv.shape[2]
    grad_b_qv = lax.dynamic_slice(small, (at + PIECES * hid + t * qv,), (qv,)).reshape(2, qv // 2)
    return (layer_out, in_grad, grad_w_qkv, grad_b_qv, grad_w_proj, sums[0], sums[1], sums[2], sums[3],
            sums[4], grad_w_in, grad_b_in, grad_w_out, sums[5])


def solution(mesh):
    in_specs = (
        P(("dp", "tensor"), None),
        P("dp"),
        P("dp", None),
        P(None, None, "tensor"),
        P(None, "tensor"),
        P("tensor", None),
        P(),
        P(),
        P(),
        P(),
        P(),
        P(None, "tensor"),
        P("tensor"),
        P("tensor", None),
        P(),
        P(("dp", "tensor"), None),
    )
    out_specs = (
        P(("dp", "tensor"), None),
        P(("dp", "tensor"), None),
        P(None, None, "tensor"),
        P(None, "tensor"),
        P("tensor", None),
        P(),
        P(),
        P(),
        P(),
        P(),
        P(None, "tensor"),
        P("tensor"),
        P("tensor", None),
        P(),
    )
    return jax.shard_map(shards, mesh=mesh, in_specs=in_specs, out_specs=out_specs, check_vma=False)
```

time: 945 us -> 587 us (0.62)
  waiting for transfers between devices: 447 us -> 181 us
  Pallas kernels: 0 us -> 97.8 us
  matrix products: 197 us -> 99.5 us
  local copies, waits for them, and re-layouts: 97.5 us -> 27.3 us
  other arithmetic: 110 us -> 44.9 us
  starting transfers between devices: 1.55 us -> 55 us
  between operations: 15 us -> 3.79 us
    psum x1 -> x0, waiting for transfers between devices: 183 us -> none  [shards(): lax.psum((grad_w_qkv, grad_b_qv, grad_w_proj, grad_w_in, grad_b_in, grad_...]
    ppermute x0 -> x54, waiting for transfers between devices: none -> 181 us  [the longest x51 154 us: swap(): lax.ppermute(v, axis, [(i, i ^ bit) for i in range(lax.axis_size(axis))])]
    all_gather x4 -> x0, waiting for transfers between devices: 140 us -> none  [the longest x1 38.3 us: shards(): attn_input_all = lax.all_gather(attn_input, 'tensor', axis=0, tiled=True)]
    reduce_scatter x4 -> x0, waiting for transfers between devices: 123 us -> none  [the longest x1 47.3 us: shards(): lax.psum_scatter(jnp.dot(context, w_proj, preferred_element_type=jnp.floa...]
    pallas_call x0 -> x4, Pallas kernels: none -> 97.8 us  [the longest x2 60.3 us: attn_bwd(): pl.pallas_call(attn_bwd_kernel, out_shape=(shape(rows), shape(prompt), sh...]
    dot_general x53 -> x56, matrix products: 193 us -> 99.5 us  [the longest x20 39.7 us: nt(): lax.dot_general(a, b, (((1,), (1,)), ((), ())), preferred_element_type=F32)]
    ppermute x0 -> x54, starting transfers between devices: none -> 55 us  [the longest x51 48.3 us: swap(): lax.ppermute(v, axis, [(i, i ^ bit) for i in range(lax.axis_size(axis))])]
    reduce_sum x26 -> x13, other arithmetic: 39.1 us -> 7.09 us  [the longest x1 3.27 us: shards(): sum_b_out = jnp.sum(dy, axis=0)]
  transfers between devices with their start and end apart: 9 -> 54, of which waited for: 8 -> 28; matrix products, arithmetic and copies ran while one was open for 8% -> 21% of each run, Pallas kernels for 0% -> 6%
where the time goes in v1:
time: 587 us; the launch traced here: 580 us
  waiting for transfers between devices  181 us (31%)
  matrix products  99.5 us (17%)
  Pallas kernels  97.8 us (17%)
  blocking collectives  70.7 us (12%)
  starting transfers between devices  55 us (9%)
  other arithmetic  44.9 us (8%)
  local copies, waits for them, and re-layouts  27.3 us (5%)
    ppermute x51, waiting for transfers between devices, swap(): lax.ppermute(v, axis, [(i, i ^ bit) for i in range(lax.axis_size(axis))])  154 us
    psum x1, blocking collectives, shards(): small = lax.psum(small, ('dp', 'tensor'))  70.7 us
    pallas_call x2, Pallas kernels, attn_bwd(): pl.pallas_call(attn_bwd_kernel, out_shape=(shape(rows), shape(prompt), sh...  60.3 us
    ppermute x51, starting transfers between devices, swap(): lax.ppermute(v, axis, [(i, i ^ bit) for i in range(lax.axis_size(axis))])  48.3 us
    dot_general x20, matrix products, nt(): lax.dot_general(a, b, (((1,), (1,)), ((), ())), preferred_element_type=F32)  39.7 us
    pallas_call x2, Pallas kernels, attn_fwd(): pl.pallas_call(attn_fwd_kernel, out_shape=(jax.ShapeDtypeStruct((rows, wi...  37.5 us
    dot_general x16, matrix products, tn(): lax.dot_general(a, b, (((0,), (0,)), ((), ())), preferred_element_type=F32)  31.2 us
    dot_general x20, matrix products, nn(): lax.dot_general(a, b, (((1,), (0,)), ((), ())), preferred_element_type=F32)  28.7 us
  transfers between devices with their start and end apart: 54, of which 28 were waited for; matrix products, arithmetic and copies ran while one was open for 21% of the time, Pallas kernels for 6%

profile of v1, /device:TPU:0, one launch (start us, length us, event | category | flops | bytes accessed | tf_op | source)
XLA Modules:
  0.0 580.5 jit_solution(16555866099096128742)
XLA Ops:
  30.0 4.0 collective-permute-done.5
  38.2 21.1 %collective-permute-done.12 = bf16[768,768]{1,0:T(8,128)(2,1)} collective-permute-done((bf16[768,768]{1,0:T(8,128)(2,1)}, bf16[768,768]{1,0:T(8,128)(2,1)}, u32[]{:S(2)}, u32[]{:S(2)}) %collective-permute-start.12) | collective-permute-done | bytes 1179680 | tf_op jit(solution)/shard_map/ppermute | solution.py:235
  59.3 4.1 collective-permute-start.2
  63.4 21.4 %collective-permute-done.11 = bf16[784,768]{1,0:T(8,128)(2,1)S(1)} collective-permute-done((bf16[784,768]{1,0:T(8,128)(2,1)}, bf16[784,768]{1,0:T(8,128)(2,1)S(1)}, u32[]{:S(2)}, u32[]{:S(2)}) %collective-permute-start.11) | collective-permute-done | bytes 1204256 | tf_op jit(solution)/shard_map/ppermute | solution.py:235
  86.5 14.4 %collective-permute-done.2 = bf16[512,768]{0,1:T(8,128)(2,1)S(1)} collective-permute-done((bf16[512,768]{0,1:T(8,128)(2,1)S(1)}, bf16[512,768]{0,1:T(8,128)(2,1)S(1)}, u32[]{:S(2)}, u32[]{:S(2)}) %collective-permute-start.2) | collective-permute-done | bytes 786464 | tf_op jit(solution)/shard_map/ppermute | solution.py:298
  109.2 18.9 %attn_fwd.2 = (bf16[768,384]{1,0:T(8,128)(2,1)S(1)}, f32[3,3,8,256]{3,2,1,0:T(8,128)S(1)}) custom-call(s32[4]{0:T(128)S(1)} %pad_add_fusion.lens, bf16[768,384]{1,0:T(8,128)(2,1)S(1)} %fusion.66.q_ref, bf16[1024,384]{1,0:T(8,128)(2,1)S(1)} %convolution_convert_fusion.5.kp_ref, bf16[1024,384]{1,0:T(8,128)(2,1)S(1)} %add_convert_fusion.6.vp_ref, ...), custom_call_target="tpu_custom_call" | custom-call | flops 6039797760 | bytes 3932160 | tf_op jit(solution)/shard_map/attn_fwd/pallas_call | solution.py:180
  128.9 18.7 %attn_fwd.3 = (bf16[768,384]{1,0:T(8,128)(2,1)S(1)}, f32[3,3,8,256]{3,2,1,0:T(8,128)S(1)}) custom-call(s32[4]{0:T(128)S(1)} %pad_add_fusion.lens, bf16[768,384]{1,0:T(8,128)(2,1)S(1)} %fusion.68.q_ref, bf16[1024,384]{1,0:T(8,128)(2,1)S(1)} %convolution_convert_fusion.4.kp_ref, bf16[1024,384]{1,0:T(8,128)(2,1)S(1)} %add_convert_fusion.5.vp_ref, ...), custom_call_target="tpu_custom_call" | custom-call | flops 6039797760 | bytes 3932160 | tf_op jit(solution)/shard_map/attn_fwd/pallas_call | solution.py:180
  170.1 3.6 convert_reduce_fusion.4
  179.7 3.8 convert_reduce_fusion.5
  191.8 30.0 %attn_bwd.3 = (bf16[768,384]{1,0:T(8,128)(2,1)S(1)}, bf16[1024,384]{1,0:T(8,128)(2,1)S(1)}, bf16[1024,384]{1,0:T(8,128)(2,1)S(1)}, bf16[768,384]{1,0:T(8,128)(2,1)S(1)}, bf16[768,384]{1,0:T(8,128)(2,1)S(1)}) custom-call(s32[4]{0:T(128)S(1)} %pad_add_fusion.lens, bf16[768,384]{1,0:T(8,128)(2,1)S(1)} %fusion.66.q_ref, ...), custom_call_target="tpu_custom_call" | custom-call | flops 15099494400 | bytes 7864320 | tf_op jit(solution)/shard_map/attn_bwd/pallas_call | solution.py:212
  229.3 30.4 %attn_bwd.2 = (bf16[768,384]{1,0:T(8,128)(2,1)S(1)}, bf16[1024,384]{1,0:T(8,128)(2,1)S(1)}, bf16[1024,384]{1,0:T(8,128)(2,1)S(1)}, bf16[768,384]{1,0:T(8,128)(2,1)S(1)}, bf16[768,384]{1,0:T(8,128)(2,1)S(1)}) custom-call(s32[4]{0:T(128)S(1)} %pad_add_fusion.lens, bf16[768,384]{1,0:T(8,128)(2,1)S(1)} %fusion.68.q_ref, ...), custom_call_target="tpu_custom_call" | custom-call | flops 15099494400 | bytes 7864320 | tf_op jit(solution)/shard_map/attn_bwd/pallas_call | solution.py:212
  309.2 5.0 collective-permute-done.29
  316.1 3.6 collective-permute-done.30
  342.1 4.6 collective-permute-done.35
  354.3 3.5 add_convert_fusion.2
  357.8 11.2 %collective-permute-done.16 = bf16[512,768]{0,1:T(8,128)(2,1)S(1)} collective-permute-done((bf16[512,768]{0,1:T(8,128)(2,1)S(1)}, bf16[512,768]{0,1:T(8,128)(2,1)S(1)}, u32[]{:S(2)}, u32[]{:S(2)}) %collective-permute-start.16) | collective-permute-done | bytes 786464 | tf_op jit(solution)/shard_map/ppermute | solution.py:395
  373.0 14.9 %collective-permute-done.20 = bf16[2304,192]{0,1:T(8,128)(2,1)S(1)} collective-permute-done((bf16[2304,192]{0,1:T(8,128)(2,1)S(1)}, bf16[2304,192]{0,1:T(8,128)(2,1)S(1)}, u32[]{:S(2)}, u32[]{:S(2)}) %collective-permute-start.20) | collective-permute-done | bytes 884768 | tf_op jit(solution)/shard_map/ppermute | solution.py:235
  393.3 3.7 fusion.19
  397.2 3.3 convert_reduce_fusion.2
  401.0 70.7 %psum.7 = f32[9216]{0:T(1024)S(1)} all-reduce(f32[9216]{0:T(1024)S(1)} %constant_dynamic-update-slice_fusion.7), channel_id=1, replica_groups=mesh['dp'=8,'tensor'=4] {'dp','tensor'}, use_global_device_ids=true, to_apply=%region_26.27 | all-reduce | flops 9216 | bytes 73728 | tf_op jit(solution)/shard_map/psum | solution.py:411
  480.0 4.6 collective-permute-done.22
  487.5 5.1 collective-permute-done.23
  494.9 5.7 collective-permute-done.24
  501.0 3.3 collective-permute-start.48
  504.3 4.2 collective-permute-done.25
  511.0 7.6 %collective-permute-done.48 = bf16[384,768]{1,0:T(8,128)(2,1)S(1)} collective-permute-done((bf16[384,768]{1,0:T(8,128)(2,1)S(1)}, bf16[384,768]{1,0:T(8,128)(2,1)S(1)}, u32[]{:S(2)}, u32[]{:S(2)}) %collective-permute-start.48) | collective-permute-done | bytes 589856 | tf_op jit(solution)/shard_map/ppermute | solution.py:235
  521.8 5.4 collective-permute-done.49
  533.5 7.5 %collective-permute-done.50 = bf16[96,768]{1,0:T(8,128)(2,1)S(1)} collective-permute-done((bf16[96,768]{1,0:T(8,128)(2,1)S(1)}, bf16[96,768]{1,0:T(8,128)(2,1)S(1)}, u32[]{:S(2)}, u32[]{:S(2)}) %collective-permute-start.50) | collective-permute-done | bytes 147488 | tf_op jit(solution)/shard_map/ppermute | solution.py:235
  544.3 4.0 collective-permute-done.51
  548.4 6.2 %collective-permute-done.43 = bf16[192,768]{1,0:T(8,128)(2,1)S(1)} collective-permute-done((bf16[192,768]{1,0:T(8,128)(2,1)S(1)}, bf16[192,768]{1,0:T(8,128)(2,1)S(1)}, u32[]{:S(2)}, u32[]{:S(2)}) %collective-permute-start.43) | collective-permute-done | bytes 294944 | tf_op jit(solution)/shard_map/ppermute | solution.py:235
  561.6 9.6 %collective-permute-done.44 = bf16[384,768]{1,0:T(8,128)(2,1)S(1)} collective-permute-done((bf16[384,768]{1,0:T(8,128)(2,1)S(1)}, bf16[384,768]{1,0:T(8,128)(2,1)S(1)}, u32[]{:S(2)}, u32[]{:S(2)}) %collective-permute-start.44) | collective-permute-done | bytes 589856 | tf_op jit(solution)/shard_map/ppermute | solution.py:235
  572.9 5.5 collective-permute-done.53
  (518 shorter events, 217.4 us)
Async XLA Ops:
  0.7 18.7 %collective-permute-start.4 = (bf16[192,768]{1,0:T(8,128)(2,1)}, bf16[192,768]{1,0:T(8,128)(2,1)}, u32[]{:S(2)}, u32[]{:S(2)}) collective-permute-start(bf16[192,768]{1,0:T(8,128)(2,1)} %param.21), channel_id=1, source_target_pairs={{0,1},{1,0},{2,3},{3,2},{4,5},{5,4},{6,7},{7,6},{8,9},{9,8},{10,11... | collective-permute-start | bytes 884744 | tf_op jit(solution)/shard_map/ppermute | solution.py:235
  1.2 12.7 %collective-permute-start.7 = (bf16[192,768]{1,0:T(8,128)(2,1)}, bf16[192,768]{1,0:T(8,128)(2,1)}, u32[]{:S(2)}, u32[]{:S(2)}) collective-permute-start(bf16[192,768]{1,0:T(8,128)(2,1)} %param.21), channel_id=1, source_target_pairs={{0,2},{1,3},{2,0},{3,1},{4,6},{5,7},{6,4},{7,5},{8,10},{9,11},{10,... | collective-permute-start | bytes 884744 | tf_op jit(solution)/shard_map/ppermute | solution.py:235
  7.1 26.9 %collective-permute-start.5 = (bf16[3,784,192]{1,2,0:T(8,128)(2,1)}, bf16[3,784,192]{1,2,0:T(8,128)(2,1)}, u32[]{:S(2)}, u32[]{:S(2)}) collective-permute-start(bf16[3,784,192]{1,2,0:T(8,128)(2,1)} %pad_maximum_fusion.3), channel_id=1, source_target_pairs={{0,2},{1,3},{2,0},{3,1},{4,6},{5,7},{6,4},{7,5},{8,10},{9,11},{10,... | collective-permute-start | bytes 2709512 | tf_op jit(solution)/shard_map/ppermute | solution.py:235
  7.2 17.2 %collective-permute-start = (bf16[3,784,192]{1,2,0:T(8,128)(2,1)}, bf16[3,784,192]{1,2,0:T(8,128)(2,1)}, u32[]{:S(2)}, u32[]{:S(2)}) collective-permute-start(bf16[3,784,192]{1,2,0:T(8,128)(2,1)} %pad_maximum_fusion.3), channel_id=1, source_target_pairs={{0,1},{1,0},{2,3},{3,2},{4,5},{5,4},{6,7},{7,6},{8,9},{9,8},{10,11... | collective-permute-start | bytes 2709512 | tf_op jit(solution)/shard_map/ppermute | solution.py:235
  8.0 28.2 %collective-permute-start.1 = (bf16[768,768]{0,1:T(8,128)(2,1)S(1)}, bf16[768,768]{0,1:T(8,128)(2,1)}, u32[]{:S(2)}, u32[]{:S(2)}) collective-permute-start(bf16[768,768]{0,1:T(8,128)(2,1)S(1)} %copy.57), channel_id=1, source_target_pairs={{0,1},{1,0},{2,3},{3,2},{4,5},{5,4},{6,7},{7,6},{8,9},{9,8},{10,11... | collective-permute-start | bytes 3538952 | tf_op jit(solution)/shard_map/ppermute | solution.py:235
  19.4 150.8 %collective-permute-start.10 = (bf16[768,768]{1,0:T(8,128)(2,1)}, bf16[768,768]{1,0:T(8,128)(2,1)}, u32[]{:S(2)}, u32[]{:S(2)}) collective-permute-start(bf16[768,768]{1,0:T(8,128)(2,1)} %param.29), channel_id=1, source_target_pairs={{0,1},{1,0},{2,3},{3,2},{4,5},{5,4},{6,7},{7,6},{8,9},{9,8},{10,11... | collective-permute-start | bytes 3538952 | tf_op jit(solution)/shard_map/ppermute | solution.py:235
  21.5 37.9 %collective-permute-start.12 = (bf16[768,768]{1,0:T(8,128)(2,1)}, bf16[768,768]{1,0:T(8,128)(2,1)}, u32[]{:S(2)}, u32[]{:S(2)}) collective-permute-start(bf16[768,768]{1,0:T(8,128)(2,1)} %param.29), channel_id=1, source_target_pairs={{0,2},{1,3},{2,0},{3,1},{4,6},{5,7},{6,4},{7,5},{8,10},{9,11},{10,... | collective-permute-start | bytes 3538952 | tf_op jit(solution)/shard_map/ppermute | solution.py:235
  24.4 60.3 %collective-permute-start.11 = (bf16[784,768]{1,0:T(8,128)(2,1)}, bf16[784,768]{1,0:T(8,128)(2,1)S(1)}, u32[]{:S(2)}, u32[]{:S(2)}) collective-permute-start(bf16[784,768]{1,0:T(8,128)(2,1)} %fusion.70), channel_id=1, source_target_pairs={{0,2},{1,3},{2,0},{3,1},{4,6},{5,7},{6,4},{7,5},{8,10},{9,11},{10,... | collective-permute-start | bytes 3612680 | tf_op jit(solution)/shard_map/ppermute | solution.py:235
  34.1 50.7 %collective-permute-start.9 = (bf16[784,768]{1,0:T(8,128)(2,1)S(1)}, bf16[784,768]{1,0:T(8,128)(2,1)S(1)}, u32[]{:S(2)}, u32[]{:S(2)}) collective-permute-start(bf16[784,768]{1,0:T(8,128)(2,1)S(1)} %copy-done.40), channel_id=1, source_target_pairs={{0,1},{1,0},{2,3},{3,2},{4,5},{5,4},{6,7},{7,6},{8,9},{9,8},{10,11... | collective-permute-start | bytes 3612680 | tf_op jit(solution)/shard_map/ppermute | solution.py:235
  36.2 49.2 %collective-permute-start.6 = (bf16[3,784,192]{1,2,0:T(8,128)(2,1)}, bf16[3,784,192]{1,2,0:T(8,128)(2,1)S(1)}, u32[]{:S(2)}, u32[]{:S(2)}) collective-permute-start(bf16[3,784,192]{1,2,0:T(8,128)(2,1)} %collective-permute-done.5), channel_id=1, source_target_pairs={{0,1},{1,0},{2,3},{3,2},{4,5},{5,4},{6,7},{7,6},{8,9},{9,8},{10,11... | collective-permute-start | bytes 2709512 | tf_op jit(solution)/shard_map/ppermute | solution.py:235
  59.3 41.6 %collective-permute-start.2 = (bf16[512,768]{0,1:T(8,128)(2,1)S(1)}, bf16[512,768]{0,1:T(8,128)(2,1)S(1)}, u32[]{:S(2)}, u32[]{:S(2)}) collective-permute-start(bf16[512,768]{0,1:T(8,128)(2,1)S(1)} %fusion.83), channel_id=1, source_target_pairs={{0,2},{1,3},{4,6},{5,7},{8,10},{9,11},{12,14},{13,15},{16,18},{17,... | collective-permute-start | bytes 2359304 | tf_op jit(solution)/shard_map/ppermute | solution.py:298
  84.8 74.1 %collective-permute-start.14 = (bf16[768,768]{1,0:T(8,128)(2,1)}, bf16[768,768]{1,0:T(8,128)(2,1)S(1)}, u32[]{:S(2)}, u32[]{:S(2)}) collective-permute-start(bf16[768,768]{1,0:T(8,128)(2,1)} %collective-permute-done.12), channel_id=1, source_target_pairs={{0,1},{1,0},{2,3},{3,2},{4,5},{5,4},{6,7},{7,6},{8,9},{9,8},{10,11... | collective-permute-start | bytes 3538952 | tf_op jit(solution)/shard_map/ppermute | solution.py:235
  84.8 18.0 %collective-permute-start.13 = (bf16[784,768]{1,0:T(8,128)(2,1)S(1)}, bf16[784,768]{1,0:T(8,128)(2,1)S(1)}, u32[]{:S(2)}, u32[]{:S(2)}) collective-permute-start(bf16[784,768]{1,0:T(8,128)(2,1)S(1)} %collective-permute-done.11), channel_id=1, source_target_pairs={{0,1},{1,0},{2,3},{3,2},{4,5},{5,4},{6,7},{7,6},{8,9},{9,8},{10,11... | collective-permute-start | bytes 3612680 | tf_op jit(solution)/shard_map/ppermute | solution.py:235
  278.0 76.2 %collective-permute-start.37 = (bf16[768,768]{1,0:T(8,128)(2,1)}, bf16[768,768]{1,0:T(8,128)(2,1)}, u32[]{:S(2)}, u32[]{:S(2)}) collective-permute-start(bf16[768,768]{1,0:T(8,128)(2,1)} %convolution_convert_fusion.2), channel_id=1, source_target_pairs={{0,1},{1,0},{2,3},{3,2},{4,5},{5,4},{6,7},{7,6},{8,9},{9,8},{10,11... | collective-permute-start | bytes 3538952 | tf_op jit(solution)/shard_map/ppermute | solution.py:235
  278.5 70.3 %collective-permute-start.46 = (bf16[768,768]{1,0:T(8,128)(2,1)}, bf16[768,768]{1,0:T(8,128)(2,1)}, u32[]{:S(2)}, u32[]{:S(2)}) collective-permute-start(bf16[768,768]{1,0:T(8,128)(2,1)} %convolution_convert_fusion), channel_id=1, source_target_pairs={{0,1},{1,0},{2,3},{3,2},{4,5},{5,4},{6,7},{7,6},{8,9},{9,8},{10,11... | collective-permute-start | bytes 3538952 | tf_op jit(solution)/shard_map/ppermute | solution.py:235
  283.6 209.3 %collective-permute-start.45 = (bf16[768,768]{1,0:T(8,128)(2,1)}, bf16[768,768]{1,0:T(8,128)(2,1)}, u32[]{:S(2)}, u32[]{:S(2)}) collective-permute-start(bf16[768,768]{1,0:T(8,128)(2,1)} %convolution_convert_fusion.1), channel_id=1, source_target_pairs={{0,1},{1,0},{2,3},{3,2},{4,5},{5,4},{6,7},{7,6},{8,9},{9,8},{10,11... | collective-permute-start | bytes 3538952 | tf_op jit(solution)/shard_map/ppermute | solution.py:235
  286.8 16.6 %collective-permute-start.28 = (bf16[192,768]{1,0:T(8,128)(2,1)}, bf16[192,768]{1,0:T(8,128)(2,1)}, u32[]{:S(2)}, u32[]{:S(2)}) collective-permute-start(bf16[192,768]{1,0:T(8,128)(2,1)} %slice.561), channel_id=1, source_target_pairs={{0,1},{1,0},{2,3},{3,2},{4,5},{5,4},{6,7},{7,6},{8,9},{9,8},{10,11... | collective-permute-start | bytes 884744 | tf_op jit(solution)/shard_map/ppermute | solution.py:235
  286.8 22.3 %collective-permute-start.27 = (bf16[192,768]{1,0:T(8,128)(2,1)S(1)}, bf16[192,768]{1,0:T(8,128)(2,1)S(1)}, u32[]{:S(2)}, u32[]{:S(2)}) collective-permute-start(bf16[192,768]{1,0:T(8,128)(2,1)S(1)} %slice.562), channel_id=1, source_target_pairs={{0,1},{1,0},{2,3},{3,2},{4,5},{5,4},{6,7},{7,6},{8,9},{9,8},{10,11... | collective-permute-start | bytes 884744 | tf_op jit(solution)/shard_map/ppermute | solution.py:235
  309.2 25.6 %collective-permute-start.15 = (bf16[512,768]{0,1:T(8,128)(2,1)}, bf16[512,768]{0,1:T(8,128)(2,1)}, u32[]{:S(2)}, u32[]{:S(2)}) collective-permute-start(bf16[512,768]{0,1:T(8,128)(2,1)} %broadcast_select_fusion.1), channel_id=1, source_target_pairs={{0,1},{1,0},{2,3},{3,2},{4,5},{5,4},{6,7},{7,6},{8,9},{9,8},{10,11... | collective-permute-start | bytes 2359304 | tf_op jit(solution)/shard_map/ppermute | solution.py:235
  340.3 30.7 %collective-permute-start.18 = (bf16[2304,192]{0,1:T(8,128)(2,1)S(1)}, bf16[2304,192]{0,1:T(8,128)(2,1)S(1)}, u32[]{:S(2)}, u32[]{:S(2)}) collective-permute-start(bf16[2304,192]{0,1:T(8,128)(2,1)S(1)} %copy-done.52), channel_id=1, source_target_pairs={{0,1},{1,0},{2,3},{3,2},{4,5},{5,4},{6,7},{7,6},{8,9},{9,8},{10,11... | collective-permute-start | bytes 2654216 | tf_op jit(solution)/shard_map/ppermute | solution.py:235
  346.7 22.3 %collective-permute-start.16 = (bf16[512,768]{0,1:T(8,128)(2,1)S(1)}, bf16[512,768]{0,1:T(8,128)(2,1)S(1)}, u32[]{:S(2)}, u32[]{:S(2)}) collective-permute-start(bf16[512,768]{0,1:T(8,128)(2,1)S(1)} %fusion.49), channel_id=1, source_target_pairs={{2,0},{3,1},{6,4},{7,5},{10,8},{11,9},{14,12},{15,13},{18,16},{19,... | collective-permute-start | bytes 2359304 | tf_op jit(solution)/shard_map/ppermute | solution.py:395
  348.9 39.1 %collective-permute-start.20 = (bf16[2304,192]{0,1:T(8,128)(2,1)S(1)}, bf16[2304,192]{0,1:T(8,128)(2,1)S(1)}, u32[]{:S(2)}, u32[]{:S(2)}) collective-permute-start(bf16[2304,192]{0,1:T(8,128)(2,1)S(1)} %fusion.47), channel_id=1, source_target_pairs={{0,2},{1,3},{2,0},{3,1},{4,6},{5,7},{6,4},{7,5},{8,10},{9,11},{10,... | collective-permute-start | bytes 2654216 | tf_op jit(solution)/shard_map/ppermute | solution.py:235
  354.2 123.7 %collective-permute-start.36 = (bf16[768,768]{1,0:T(8,128)(2,1)}, bf16[768,768]{1,0:T(8,128)(2,1)}, u32[]{:S(2)}, u32[]{:S(2)}) collective-permute-start(bf16[768,768]{1,0:T(8,128)(2,1)} %convolution_convert_fusion.3), channel_id=1, source_target_pairs={{0,1},{1,0},{2,3},{3,2},{4,5},{5,4},{6,7},{7,6},{8,9},{9,8},{10,11... | collective-permute-start | bytes 3538952 | tf_op jit(solution)/shard_map/ppermute | solution.py:235
  369.0 123.9 %collective-permute-start.47 = (bf16[768,768]{1,0:T(8,128)(2,1)}, bf16[768,768]{1,0:T(8,128)(2,1)}, u32[]{:S(2)}, u32[]{:S(2)}) collective-permute-start(bf16[768,768]{1,0:T(8,128)(2,1)} %add_convert_fusion.1), channel_id=1, source_target_pairs={{0,2},{1,3},{2,0},{3,1},{4,6},{5,7},{6,4},{7,5},{8,10},{9,11},{10,... | collective-permute-start | bytes 3538952 | tf_op jit(solution)/shard_map/ppermute | solution.py:235
  371.0 107.0 %collective-permute-start.38 = (bf16[768,768]{1,0:T(8,128)(2,1)}, bf16[768,768]{1,0:T(8,128)(2,1)}, u32[]{:S(2)}, u32[]{:S(2)}) collective-permute-start(bf16[768,768]{1,0:T(8,128)(2,1)} %add_convert_fusion.2), channel_id=1, source_target_pairs={{0,2},{1,3},{2,0},{3,1},{4,6},{5,7},{6,4},{7,5},{8,10},{9,11},{10,... | collective-permute-start | bytes 3538952 | tf_op jit(solution)/shard_map/ppermute | solution.py:235
  391.6 84.7 %collective-permute-start.21 = (bf16[1152,192]{0,1:T(8,128)(2,1)S(1)}, bf16[1152,192]{0,1:T(8,128)(2,1)}, u32[]{:S(2)}, u32[]{:S(2)}) collective-permute-start(bf16[1152,192]{0,1:T(8,128)(2,1)S(1)} %select_convert_fusion.2), channel_id=1, source_target_pairs={{0,4},{4,0},{8,12},{12,8},{16,20},{20,16},{24,28},{28,24},{1,5},{5... | collective-permute-start | bytes 1327112 | tf_op jit(solution)/shard_map/ppermute | solution.py:235
  485.9 24.8 %collective-permute-start.39 = (bf16[384,768]{1,0:T(8,128)(2,1)S(1)}, bf16[384,768]{1,0:T(8,128)(2,1)S(1)}, u32[]{:S(2)}, u32[]{:S(2)}) collective-permute-start(bf16[384,768]{1,0:T(8,128)(2,1)S(1)} %select_convert_fusion.1), channel_id=1, source_target_pairs={{0,4},{4,0},{8,12},{12,8},{16,20},{20,16},{24,28},{28,24},{1,5},{5... | collective-permute-start | bytes 1769480 | tf_op jit(solution)/shard_map/ppermute | solution.py:235
  501.0 17.6 %collective-permute-start.48 = (bf16[384,768]{1,0:T(8,128)(2,1)S(1)}, bf16[384,768]{1,0:T(8,128)(2,1)S(1)}, u32[]{:S(2)}, u32[]{:S(2)}) collective-permute-start(bf16[384,768]{1,0:T(8,128)(2,1)S(1)} %select_convert_fusion), channel_id=1, source_target_pairs={{0,4},{4,0},{8,12},{12,8},{16,20},{20,16},{24,28},{28,24},{1,5},{5... | collective-permute-start | bytes 1769480 | tf_op jit(solution)/shard_map/ppermute | solution.py:235
  508.8 21.5 %collective-permute-start.26 = (bf16[1152,192]{0,1:T(8,128)(2,1)S(1)}, bf16[1152,192]{0,1:T(8,128)(2,1)S(1)}, u32[]{:S(2)}, u32[]{:S(2)}) collective-permute-start(bf16[1152,192]{0,1:T(8,128)(2,1)S(1)} %pad_maximum_fusion.8), channel_id=1, source_target_pairs={{0,4},{4,0},{8,12},{12,8},{16,20},{20,16},{24,28},{28,24},{1,5},{5... | collective-permute-start | bytes 1327112 | tf_op jit(solution)/shard_map/ppermute | solution.py:235
  527.3 13.7 %collective-permute-start.50 = (bf16[96,768]{1,0:T(8,128)(2,1)S(1)}, bf16[96,768]{1,0:T(8,128)(2,1)S(1)}, u32[]{:S(2)}, u32[]{:S(2)}) collective-permute-start(bf16[96,768]{1,0:T(8,128)(2,1)S(1)} %select_convert_fusion.6), channel_id=1, source_target_pairs={{0,16},{4,20},{8,24},{12,28},{16,0},{20,4},{24,8},{28,12},{1,17},{... | collective-permute-start | bytes 442376 | tf_op jit(solution)/shard_map/ppermute | solution.py:235
  554.8 16.3 %collective-permute-start.44 = (bf16[384,768]{1,0:T(8,128)(2,1)S(1)}, bf16[384,768]{1,0:T(8,128)(2,1)S(1)}, u32[]{:S(2)}, u32[]{:S(2)}) collective-permute-start(bf16[384,768]{1,0:T(8,128)(2,1)S(1)} %pad_maximum_fusion.6), channel_id=1, source_target_pairs={{0,4},{4,0},{8,12},{12,8},{16,20},{20,16},{24,28},{28,24},{1,5},{5... | collective-permute-start | bytes 1769480 | tf_op jit(solution)/shard_map/ppermute | solution.py:235
  558.9 19.5 %collective-permute-start.53 = (bf16[384,768]{1,0:T(8,128)(2,1)S(1)}, bf16[384,768]{1,0:T(8,128)(2,1)S(1)}, u32[]{:S(2)}, u32[]{:S(2)}) collective-permute-start(bf16[384,768]{1,0:T(8,128)(2,1)S(1)} %pad_maximum_fusion.7), channel_id=1, source_target_pairs={{0,4},{4,0},{8,12},{12,8},{16,20},{20,16},{24,28},{28,24},{1,5},{5... | collective-permute-start | bytes 1769480 | tf_op jit(solution)/shard_map/ppermute | solution.py:235
  (131 other events, 1521.3 us)

commit v2 on v1

v2 whole, which is shorter than its diff:
```python
import functools

import jax
import jax.numpy as jnp
from jax import lax
from jax.experimental import pallas as pl
from jax.experimental.pallas import tpu as pltpu
from jax.sharding import PartitionSpec as P

HEAD = 64
PROMPT = 1024
CONT = 8
CLEN = 256
PIECES = 4
MESH = pl.DeviceIdType.MESH
ANY = pl.BlockSpec(memory_space=pl.ANY)

EPS = 1e-06
MASKED = -1000000000.0
BF = jnp.bfloat16
F32 = jnp.float32


def nt(a, b):
    return lax.dot_general(a, b, (((1,), (1,)), ((), ())), preferred_element_type=F32)


def nn(a, b):
    return lax.dot_general(a, b, (((1,), (0,)), ((), ())), preferred_element_type=F32)


def tn(a, b):
    return lax.dot_general(a, b, (((0,), (0,)), ((), ())), preferred_element_type=F32)


class Peers:
    def __init__(self):
        self.t = lax.axis_index("tensor")
        self.d = lax.axis_index("dp")
        self.odd = lax.rem(self.t, 2)
        self.p = lax.rem(self.d, 2)
        self.z = lax.div(self.d, 2)
        self.core = {"tensor": self.t + 1 - 2 * self.odd}
        self.x = {"tensor": lax.rem(self.t + 2, 4)}
        self.y = {"dp": self.d + 1 - 2 * self.p}

    def along(self, k, count):
        return {"dp": lax.rem(self.z + k, count) * 2 + self.p}


def enter(devices):
    barrier = pltpu.get_barrier_semaphore()
    for device in devices:
        pl.semaphore_signal(barrier, inc=1, device_id=device, device_id_type=MESH)
    pl.semaphore_wait(barrier, len(devices))


def remote(src, dst, send, recv, device):
    return pltpu.make_async_remote_copy(
        src_ref=src, dst_ref=dst, send_sem=send, recv_sem=recv, device_id=device, device_id_type=MESH
    )


def split_rows(rows, parts, most):
    best = None
    for count in range(most, 0, -1):
        step = count * parts * 8
        padded = -(-rows // step) * step
        if best is None or padded < best[0]:
            best = (padded, count)
    padded, count = best
    return count, padded // count // parts


def part_of(parts):
    return [2 * (k % (parts // 2)) + k // (parts // 2) for k in range(parts)]


STAGES = 7


def sum_scratch(chunks, parts, rows, width):
    half = parts // 2

    def buf(n, dtype=BF):
        return pltpu.VMEM((chunks, n, rows, width), dtype)

    def dma(n):
        return pltpu.SemaphoreType.DMA((chunks, n))

    return [
        buf(parts), buf(parts), buf(parts), buf(parts), buf(parts),
        buf(half, F32), buf(half), buf(half), buf(half), buf(half), buf(parts),
        dma(2), dma(2), dma(2), dma(2), dma(2), dma(half), dma(half), dma(half), dma(half), dma(2),
    ]


def sum_stages(me, half, g, scratch):
    (g0, g2, r1, r3, xr, keep, ysend, yr, zsend, zr, fin,
     local, core_s, core_r, xs, ys, zs, zrs, fs, frs, gs) = scratch

    def from_core(c, i):
        return remote(g.at[1 + 2 * i, c], (r1, r3)[i].at[c], core_s.at[c, i], core_r.at[c, i], me.core)

    def own(c, i):
        return pltpu.make_async_copy(g.at[2 * i, c], (g0, g2)[i].at[c], local.at[c, i])

    def across(c):
        return remote(g2.at[c], xr.at[c], xs.at[c, 0], xs.at[c, 1], me.x)

    def pair(c):
        return remote(ysend.at[c], yr.at[c], ys.at[c, 0], ys.at[c, 1], me.y)

    def rest(c, k):
        return remote(zsend.at[c, lax.rem(me.z + k, half)], zr.at[c, k], zs.at[c, k], zrs.at[c, k], me.along(k, half))

    def back(c, k):
        spot = fin.at[c, me.p * half + me.z]
        return remote(spot, spot, fs.at[c, k], frs.at[c, k], me.along(k, half))

    def back_pair(c):
        spot = fin.at[c, pl.ds(me.p * half, half)]
        return remote(spot, spot, gs.at[c, 0], gs.at[c, 1], me.y)

    def start(c):
        for i in (1, 0):
            from_core(c, i).start()
            own(c, i).start()

    def to_chip(c):
        from_core(c, 1).wait()
        own(c, 1).wait()
        g2[c] = (g2[c].astype(F32) + r3[c].astype(F32)).astype(BF)
        across(c).start()

    def to_pair(c):
        from_core(c, 0).wait()
        own(c, 0).wait()
        across(c).wait()

        def total(first):
            s = pl.ds(first, half)
            return g0[c, s].astype(F32) + r1[c, s].astype(F32) + xr[c, s].astype(F32)

        ysend[c] = total((1 - me.p) * half).astype(BF)
        pair(c).start()
        keep[c] = total(me.p * half)

    def to_rest(c):
        pair(c).wait()
        total = keep[c] + yr[c].astype(F32)
        keep[c] = total
        zsend[c] = total.astype(BF)
        for k in range(1, half):
            rest(c, k).start()

    def to_back(c):
        total = keep[c, me.z]
        for k in range(1, half):
            rest(c, k).wait()
            total = total + zr[c, k].astype(F32)
        fin[c, me.p * half + me.z] = total.astype(BF)
        for k in range(1, half):
            back(c, k).start()

    def to_back_pair(c):
        for k in range(1, half):
            back(c, k).wait()
        back_pair(c).start()

    def finish(c):
        back_pair(c).wait()

    return [start, to_chip, to_pair, to_rest, to_back, to_back_pair, finish]


def sum_peers(me, half):
    return [me.core, me.x, me.y] + [me.along(k, half) for k in range(1, half)]


def progress(stages, chunks, plan, slot):
    for s in range(STAGES - 1, 0, -1):
        first, step = plan[s]
        since = slot - first
        c = lax.div(since, step)

        @pl.when(jnp.logical_and(jnp.logical_and(since >= 0, lax.rem(since, step) == 0), c < chunks))
        def _():
            stages[s](c)


def plan_end(chunks, plan):
    return max(plan[s][0] + plan[s][1] * (chunks - 1) for s in range(1, STAGES)) + 1


def own_lanes(rows, h):
    lane = lax.broadcasted_iota(jnp.int32, (rows, 128), 1)
    return ((lane < 64) if h == 0 else (lane >= 64)), lane - (64 if h == 0 else 0)


def key_aug(k, h, length, base):
    rows = k.shape[0]
    own, extra = own_lanes(rows, h)
    row = lax.broadcasted_iota(jnp.int32, (rows, 128), 0) + base
    bias = jnp.where(jnp.logical_and(extra == 0, row >= length), MASKED, 0.0)
    return jnp.where(own, k.astype(F32), bias).astype(BF)


def query_aug(q, h):
    own, extra = own_lanes(q.shape[0], h)
    return jnp.where(own, q.astype(F32) * 0.125, jnp.where(extra == 0, 1.0, 0.0)).astype(BF)


def value_aug(v, h):
    own, extra = own_lanes(v.shape[0], h)
    ones = jnp.where(jnp.logical_and(extra >= 0, extra < 3), 1.0, 0.0)
    return jnp.where(own, v.astype(F32), ones).astype(BF)


def transposed(v):
    return v.astype(F32).T


def attn_specs(rows, prompt, blocks):
    def col(n):
        return pl.BlockSpec((n, 128), lambda i, l: (0, i))

    logs = pl.BlockSpec((1, blocks, 8, CLEN), lambda i, l: (i, 0, 0, 0))
    return col(rows), col(prompt), logs


class Weight:
    def __init__(self, me, own, spots, view, sems):
        self.me, self.own, self.spots, self.view = me, own, spots, view
        self.send, self.recv = sems

    def side(self):
        return remote(self.own, self.spots(1), self.send.at[0], self.recv.at[0], self.me.core)

    def across(self):
        p = self.me.p
        return remote(self.view(None, p), self.view(2, p), self.send.at[1], self.recv.at[1], self.me.x)

    def pair(self):
        p = self.me.p
        return remote(self.view(2, p), self.view(2, p), self.send.at[2], self.recv.at[2], self.me.y)

    def over(self, which):
        h = self.me.p if which == 0 else 1 - self.me.p
        return remote(self.view(2, h), self.view(3, h), self.send.at[3 + which], self.recv.at[3 + which], self.me.core)

    def start(self):
        self.side().start()
        self.across().start()

    def relay(self):
        self.across().wait_recv()
        self.pair().start()
        self.over(0).start()

    def relay_pair(self):
        self.pair().wait_recv()
        self.over(1).start()

    def finish(self):
        self.side().wait()
        self.across().wait_send()
        self.pair().wait_send()
        self.over(0).wait()
        self.over(1).wait()


def norm_rows(x, gain, shift):
    x = x.astype(F32)
    centred = x - jnp.mean(x, axis=-1, keepdims=True)
    scale = lax.rsqrt(jnp.mean(centred * centred, axis=-1, keepdims=True) + EPS)
    return (centred * scale * gain + shift).astype(BF)


def front_kernel(lens, x_ref, gain_ref, shift_ref, wq, wp, wi, wo, ws,
                 q_ref, kp_ref, vp_ref, ko_ref, vo_ref, ctx_ref, lse_ref, an_ref, anp_ref,
                 wq_all, wp_all, wi_all, wo_all, ws_all,
                 px, wv, wsv, kph, vpt, px_s, px_r, send, recv, loc):
    me = Peers()
    step = pl.program_id(0)
    rows = x_ref.shape[0]
    blocks = rows // CLEN
    prompt = px.shape[0]
    part = wq.shape[1]
    own_chunks = rows // CLEN
    chunks = prompt // CLEN

    def qkv_view(r, h):
        n = part // 2
        if r is None:
            return wq.at[:, pl.ds(h * n, n)]
        return wv.at[:, pl.ds(r * part + h * n, n)]

    def plain(own, everything):
        n = own.shape[0] // 2

        def view(r, h):
            return own.at[pl.ds(h * n, n)] if r is None else everything.at[r, pl.ds(h * n, n)]

        return view

    def weight(i, own, everything):
        return Weight(me, own, lambda r: everything.at[r], plain(own, everything), (send.at[i], recv.at[i]))

    w_qkv = Weight(me, wq, lambda r: wv.at[:, pl.ds(r * part, part)], qkv_view, (send.at[0], recv.at[0]))
    w_small = weight(1, ws, wsv)
    w_proj = weight(2, wp, wp_all)
    w_in = weight(3, wi, wi_all)
    w_out = weight(4, wo, wo_all)
    later = [w_proj, w_in, w_out]

    def keep(own, spot, i):
        return pltpu.make_async_copy(own, spot, loc.at[i])

    mine = [
        keep(wq, wv.at[:, pl.ds(0, part)], 0), keep(ws, wsv.at[0], 1), keep(wp, wp_all.at[0], 2),
        keep(wi, wi_all.at[0], 3), keep(wo, wo_all.at[0], 4), keep(wv, wq_all, 5), keep(wsv, ws_all, 6),
    ]

    def chunk(k):
        return px.at[pl.ds(k * CLEN, CLEN)]

    def held(k):
        at = k if k < own_chunks else k - own_chunks
        return x_ref.at[pl.ds(at * CLEN, CLEN)]

    def hop(k, src, n, device):
        return remote(src, chunk(k), px_s.at[n, k], px_r.at[n, k], device)

    first = [k for k in range(chunks) if k < own_chunks]
    second = [k for k in range(chunks) if k >= own_chunks]
    low = [k for k in range(chunks) if k < chunks // 2]
    high = second + [k for k in range(chunks // 2, own_chunks)]

    def normed(k):
        anp_ref[k * CLEN : (k + 1) * CLEN, :] = norm_rows(px[k * CLEN : (k + 1) * CLEN, :], gain_ref[...], shift_ref[...])

    @pl.when(step == 0)
    def _():
        enter([me.core, me.x, me.y])

        @pl.when(me.t == 0)
        def _():
            for k in low:
                hop(k, held(k), 1, me.x).start()
            for k in reversed(first):
                hop(k, held(k), 0, me.core).start()

        @pl.when(me.t == 1)
        def _():
            for k in second:
                hop(k, held(k), 1, me.x).start()
                hop(k, held(k), 0, me.core).start()

        for w in (w_qkv, w_small):
            w.side().start()
        for i in range(5):
            mine[i].start()

        @pl.when(me.t == 1)
        def _():
            for k in reversed(first):
                hop(k, held(k), 0, me.core).wait_recv()
                if k in high:
                    hop(k, chunk(k), 1, me.x).start()

        for w in (w_qkv, w_small):
            w.across().start()
        for w in later:
            w.side().start()
        for b in range(blocks):
            an_ref[b * CLEN : (b + 1) * CLEN, :] = norm_rows(x_ref[b * CLEN : (b + 1) * CLEN, :], gain_ref[...], shift_ref[...])

        @pl.when(me.t == 0)
        def _():
            for k in first:
                px[k * CLEN : (k + 1) * CLEN, :] = x_ref[k * CLEN : (k + 1) * CLEN, :]
            for k in second:
                hop(k, held(k), 0, me.core).wait_recv()
            for k in first:
                hop(k, held(k), 0, me.core).wait_send()
            for k in low:
                hop(k, held(k), 1, me.x).wait_send()

        @pl.when(me.t == 1)
        def _():
            for k in second:
                px[k * CLEN : (k + 1) * CLEN, :] = held(k)[...]
                hop(k, held(k), 0, me.core).wait_send()
            for k in high:
                hop(k, chunk(k), 1, me.x).wait_send()

        @pl.when(me.t == 2)
        def _():
            for k in low:
                hop(k, chunk(k), 1, me.x).wait_recv()
                hop(k, chunk(k), 0, me.core).start()
            for k in high:
                hop(k, chunk(k), 0, me.core).wait_recv()
            for k in low:
                hop(k, chunk(k), 0, me.core).wait_send()

        @pl.when(me.t == 3)
        def _():
            for k in high:
                hop(k, chunk(k), 1, me.x).wait_recv()
                hop(k, chunk(k), 0, me.core).start()
            for k in low:
                hop(k, chunk(k), 0, me.core).wait_recv()
            for k in high:
                hop(k, chunk(k), 0, me.core).wait_send()

        for k in range(chunks):
            normed(k)
        w_small.relay()
        for w in (w_qkv, w_small):
            w.side().wait_recv()
        for i in range(2):
            mine[i].wait()

    @pl.when(step == 3)
    def _():
        for w in (w_qkv, w_small):
            w.over(0).wait_recv()
            w.over(1).wait_recv()
        mine[5].start()
        mine[6].start()

    def moves(slot):
        def at(k, *steps):
            @pl.when(slot == k)
            def _():
                for s in steps:
                    s()

        at(2, w_qkv.relay, *[lambda w=w: w.across().start() for w in later])
        at(6, w_qkv.relay_pair, w_small.relay_pair)
        at(9, w_proj.relay)
        at(11, w_proj.relay_pair)
        at(13, w_in.relay)
        at(16, w_in.relay_pair)

    pick = pl.ds(pl.multiple_of(step * 128, 128), 128)
    w3 = jnp.concatenate([wv[0, pick], wv[1, pick], wv[2, pick]], axis=0)
    u = 2 * lax.div(step, 3)
    left = wsv[u, :16, pick].astype(F32)
    right = wsv[u + 1, :16, pick].astype(F32)
    spot = lax.broadcasted_iota(jnp.int32, left.shape, 0)

    def bias(k):
        return jnp.sum(jnp.where(spot == u + k, left, 0.0) + jnp.where(spot == u + 1 + k, right, 0.0), axis=0, keepdims=True)

    bq = bias(0)
    bv = bias(PIECES)
    for b in range(blocks):
        at = slice(b * CLEN, (b + 1) * CLEN)
        got = nt(an_ref[at, :], w3)
        q_ref[at, :] = (got[:, :128] + bq).astype(BF)
        ko_ref[at, :] = got[:, 128:256].astype(BF)
        vo_ref[at, :] = (got[:, 256:] + bv).astype(BF)
    for c in range(chunks):
        at = slice(c * CLEN, (c + 1) * CLEN)
        got = nt(anp_ref[at, :], w3[128:])
        kp_ref[at, :] = got[:, :128].astype(BF)
        vp_ref[at, :] = (got[:, 128:] + bv).astype(BF)

    vt = transposed(vp_ref[...])
    for h in range(2):
        kph[h] = key_aug(kp_ref[...], h, lens[0], 0)
        vpt[h] = jnp.concatenate([vt[64 * h : 64 * h + 64].astype(BF), jnp.ones((16, prompt), BF)], axis=0)

    def block(b, _):
        moves(step * blocks + b)
        at = pl.ds(pl.multiple_of(b * CLEN, CLEN), CLEN)
        q = q_ref[at, :]
        ko = ko_ref[at, :]
        vot = transposed(vo_ref[at, :])
        outs, logs = [], []
        for h in range(2):
            qh = query_aug(q, h)
            vh = jnp.concatenate([vot[64 * h : 64 * h + 64].astype(BF), jnp.ones((16, CLEN), BF)], axis=0)
            sp = nt(kph[h], qh)
            so = nt(key_aug(ko, h, lens[1 + b], 0), qh)
            top = jnp.maximum(jnp.max(sp, axis=0, keepdims=True), jnp.max(so, axis=0, keepdims=True))
            pp = jnp.exp(sp - top).astype(BF)
            po = jnp.exp(so - top).astype(BF)
            ot = nn(vpt[h], pp) + nn(vh, po)
            total = ot[64:65]
            outs.append(ot[:64] * (1.0 / total))
            logs.append(top + jnp.log(total))
        ctx_ref[at, :] = jnp.concatenate(outs, axis=0).T.astype(BF)
        lse_ref[0, b] = jnp.concatenate(logs + [jnp.zeros((6, CLEN), F32)], axis=0)
        return 0

    lax.fori_loop(0, blocks, block, 0)

    @pl.when(step == pl.num_programs(0) - 1)
    def _():
        w_out.relay()
        w_out.relay_pair()
        for w in [w_qkv, w_small]:
            w.side().wait_send()
            w.across().wait_send()
            w.pair().wait_send()
            w.over(0).wait_send()
            w.over(1).wait_send()
        for w in later:
            w.finish()
        for i in range(2, 7):
            mine[i].wait()


def front_call(lens, x, gain, shift, wq, wp, wi, wo, ws):
    rows, width = x.shape
    blocks = rows // CLEN
    pairs = width // 128
    r, p, logs = attn_specs(rows, PROMPT, blocks)
    cells = rows * (PROMPT + CLEN) * pairs * 2

    def whole(n):
        return pl.BlockSpec((n, width), lambda i, l: (0, 0))

    def shape(*s):
        return jax.ShapeDtypeStruct(s, BF)

    part = wq.shape[1]
    return pl.pallas_call(
        front_kernel,
        out_shape=(
            shape(rows, width), shape(PROMPT, width), shape(PROMPT, width), shape(rows, width), shape(rows, width),
            shape(rows, width), jax.ShapeDtypeStruct((pairs, blocks, 8, CLEN), F32),
            shape(rows, width), shape(PROMPT, width),
            shape(3, PIECES * part, width), shape(PIECES, *wp.shape), shape(PIECES, *wi.shape),
            shape(PIECES, *wo.shape), shape(PIECES, *ws.shape),
        ),
        grid_spec=pltpu.PrefetchScalarGridSpec(
            num_scalar_prefetch=1,
            grid=(pairs,),
            in_specs=[whole(rows), whole(1), whole(1), ANY, ANY, ANY, ANY, ANY],
            out_specs=[r, p, p, r, r, r, logs, whole(rows), whole(PROMPT), ANY, ANY, ANY, ANY, ANY],
            scratch_shapes=[
                pltpu.VMEM((PROMPT, width), BF),
                pltpu.VMEM((3, PIECES * part, width), BF),
                pltpu.VMEM((PIECES,) + ws.shape, BF),
                pltpu.VMEM((2, PROMPT, 128), BF),
                pltpu.VMEM((2, 80, PROMPT), BF),
                pltpu.SemaphoreType.DMA((2, PROMPT // CLEN)),
                pltpu.SemaphoreType.DMA((2, PROMPT // CLEN)),
                pltpu.SemaphoreType.DMA((5, 5)),
                pltpu.SemaphoreType.DMA((5, 5)),
                pltpu.SemaphoreType.DMA((7,)),
            ],
        ),
        compiler_params=pltpu.CompilerParams(collective_id=0, has_side_effects=True, vmem_limit_bytes=48 << 20),
        cost_estimate=pl.CostEstimate(flops=cells * 256 * 4, transcendentals=cells, bytes_accessed=4 << 20),
        name="front",
    )(lens, x, gain, shift, wq, wp, wi, wo, ws)


BACK_PLAN = {1: (1, 1), 2: (5, 3), 3: (7, 3), 4: (9, 3), 5: (11, 3), 6: (13, 3)}


def attn_bwd_kernel(chunks_g, half, lens, q_ref, kp_ref, vp_ref, ko_ref, vo_ref, do_ref, ctx_ref, lse_ref, g,
                    dq_ref, dkp_ref, dvp_ref, dko_ref, dvo_ref, g_out, qh_s, doh_s, dqt, out_sem, *scratch):
    me = Peers()
    step = pl.program_id(0)
    stages = sum_stages(me, half, g, scratch)

    @pl.when(step == 0)
    def _():
        enter(sum_peers(me, half))
        for c in range(chunks_g):
            stages[0](c)

    rows_all = q_ref.shape[0]
    blocks = rows_all // CLEN
    chunks = kp_ref.shape[0] // CLEN
    prod = do_ref[...].astype(F32) * ctx_ref[...].astype(F32)
    for h in range(2):
        own, extra = own_lanes(rows_all, h)
        qh_s[h] = query_aug(q_ref[...], h)
        d = -jnp.sum(jnp.where(own, prod, 0.0), axis=1, keepdims=True)
        hi = d.astype(BF).astype(F32)
        mid = (d - hi).astype(BF).astype(F32)
        low = d - hi - mid
        aug = jnp.where(extra == 0, hi, jnp.where(extra == 1, mid, jnp.where(extra == 2, low, 0.0)))
        doh_s[h] = jnp.where(own, do_ref[...].astype(F32), aug).astype(BF)
    first = lax.broadcasted_iota(jnp.int32, (CLEN, 128), 1) < 64

    def own_block(b, _):
        rows = pl.ds(pl.multiple_of(b * CLEN, CLEN), CLEN)
        q = q_ref[rows, :]
        k = ko_ref[rows, :]
        v = vo_ref[rows, :]
        do = do_ref[rows, :]
        kt = transposed(k).astype(BF)
        dks, dvs, dqs = [], [], []
        for h in range(2):
            s = nt(key_aug(k, h, lens[1 + b], 0), qh_s[h, rows, :])
            p = jnp.exp(s - lse_ref[0, b, h : h + 1, :])
            dp = nt(value_aug(v, h), doh_s[h, rows, :])
            ds = (p * dp).astype(BF)
            dvs.append(nn(p.astype(BF), do))
            dks.append(nn(ds, q))
            dqs.append(nn(kt[64 * h : 64 * h + 64], ds))
        dvo_ref[rows, :] = jnp.where(first, dvs[0], dvs[1]).astype(BF)
        dko_ref[rows, :] = (jnp.where(first, dks[0], dks[1]) * 0.125).astype(BF)
        dqt[b] = jnp.concatenate(dqs, axis=0)
        return 0

    lax.fori_loop(0, blocks, own_block, 0)

    def chunk(c, _):
        progress(stages, chunks_g, BACK_PLAN, step * chunks + c)
        rows = pl.ds(pl.multiple_of(c * CLEN, CLEN), CLEN)
        k = kp_ref[rows, :]
        v = vp_ref[rows, :]
        kt = transposed(k).astype(BF)
        dks, dvs = [], []
        for h in range(2):
            kh = key_aug(k, h, lens[0], c * CLEN)
            vh = value_aug(v, h)
            dk = dv = None
            for b in range(blocks):
                rb = pl.ds(b * CLEN, CLEN)
                s = nt(kh, qh_s[h, rb, :])
                p = jnp.exp(s - lse_ref[0, b, h : h + 1, :])
                dp = nt(vh, doh_s[h, rb, :])
                ds = (p * dp).astype(BF)
                dv_b = nn(p.astype(BF), do_ref[rb, :])
                dk_b = nn(ds, q_ref[rb, :])
                dv = dv_b if b == 0 else dv + dv_b
                dk = dk_b if b == 0 else dk + dk_b
                dqt[b, 64 * h : 64 * h + 64] += nn(kt[64 * h : 64 * h + 64], ds)
            dvs.append(dv)
            dks.append(dk)
        dvp_ref[rows, :] = jnp.where(first, dvs[0], dvs[1]).astype(BF)
        dkp_ref[rows, :] = (jnp.where(first, dks[0], dks[1]) * 0.125).astype(BF)
        return 0

    lax.fori_loop(0, chunks, chunk, 0)
    for b in range(blocks):
        dq_ref[b * CLEN : (b + 1) * CLEN, :] = (dqt[b].T * 0.125).astype(BF)

    @pl.when(step == pl.num_programs(0) - 1)
    def _():
        def more(slot, _):
            progress(stages, chunks_g, BACK_PLAN, slot)
            return 0

        lax.fori_loop(chunks * pl.num_programs(0), plan_end(chunks_g, BACK_PLAN), more, 0)
        done = pltpu.make_async_copy(scratch[10], g_out, out_sem)
        done.start()
        done.wait()


def attn_bwd(lens, q, kp, vp, ko, vo, do, ctx, lse, g):
    rows, width = q.shape
    prompt = kp.shape[0]
    blocks = rows // CLEN
    pairs = width // 128
    r, p, logs = attn_specs(rows, prompt, blocks)
    cells = rows * (prompt + CLEN) * pairs * 2
    _, count, parts, part_rows, _ = g.shape

    def shape(n):
        return jax.ShapeDtypeStruct((n, width), BF)

    return pl.pallas_call(
        functools.partial(attn_bwd_kernel, count, parts // 2),
        out_shape=(shape(rows), shape(prompt), shape(prompt), shape(rows), shape(rows),
                   jax.ShapeDtypeStruct(g.shape[1:], BF)),
        grid_spec=pltpu.PrefetchScalarGridSpec(
            num_scalar_prefetch=1,
            grid=(pairs,),
            in_specs=[r, p, p, r, r, r, r, logs, ANY],
            out_specs=[r, p, p, r, r, ANY],
            scratch_shapes=[
                pltpu.VMEM((2, rows, 128), BF),
                pltpu.VMEM((2, rows, 128), BF),
                pltpu.VMEM((blocks, 128, CLEN), F32),
                pltpu.SemaphoreType.DMA,
            ] + sum_scratch(count, parts, part_rows, width),
        ),
        compiler_params=pltpu.CompilerParams(collective_id=1, has_side_effects=True, vmem_limit_bytes=60 << 20),
        cost_estimate=pl.CostEstimate(
            flops=cells * 256 * 10, transcendentals=cells, bytes_accessed=2 * width * (8 * rows + 4 * prompt)
        ),
        name="attn_bwd",
    )(lens, q, kp, vp, ko, vo, do, ctx, lse, g)


def last_kernel(chunks_g, half, g, share, g_out, ex_out, mine, came, total, over, ex, ps, pr, loc, *scratch):
    me = Peers()
    stages = sum_stages(me, half, g, scratch)
    n = mine.shape[0]
    rows = ex.shape[0]
    spare = rows - n
    first = me.t < 2

    enter(sum_peers(me, half))
    side = remote(share.at[pl.ds((1 - me.odd) * n, n)], came, ps.at[0], pr.at[0], me.core)
    own = pltpu.make_async_copy(share.at[pl.ds(me.odd * n, n)], mine, loc.at[0])
    across = remote(total, over, ps.at[1], pr.at[1], me.x)
    end = remote(total.at[pl.ds(0, spare)], ex.at[pl.ds(n, spare)], ps.at[2], pr.at[2], me.core)
    own.start()
    side.start()
    for c in range(chunks_g):
        stages[0](c)
    own.wait()
    side.wait()
    total[...] = (mine[...].astype(F32) + came[...].astype(F32)).astype(BF)

    @pl.when(me.t >= 2)
    def _():
        across.start()
        ex[...] = jnp.zeros_like(ex)

    def run(lo, hi):
        def more(slot, _):
            progress(stages, chunks_g, LAST_PLAN, slot)
            return 0

        lax.fori_loop(lo, hi, more, 0)

    cut = chunks_g + 1
    run(0, cut)

    @pl.when(first)
    def _():
        across.wait_recv()
        total[...] = (total[...].astype(F32) + over[...].astype(F32)).astype(BF)

        @pl.when(me.t == 1)
        def _():
            end.start()
            ex[: n - spare] = total[spare:]
            ex[n - spare :] = jnp.zeros((rows - n + spare, ex.shape[1]), BF)

        @pl.when(me.t == 0)
        def _():
            ex[:n] = total[...]

    run(cut, plan_end(chunks_g, LAST_PLAN))

    @pl.when(me.t >= 2)
    def _():
        across.wait_send()

    @pl.when(me.t == 1)
    def _():
        end.wait_send()

    @pl.when(me.t == 0)
    def _():
        end.wait_recv()

    outs = [pltpu.make_async_copy(scratch[10], g_out, loc.at[1]), pltpu.make_async_copy(ex, ex_out, loc.at[2])]
    for o in outs:
        o.start()
    for o in outs:
        o.wait()


LAST_PLAN = {1: (0, 1), 2: (1, 1), 3: (2, 1), 4: (3, 1), 5: (4, 1), 6: (5, 1)}


def last_call(g, share, rows):
    _, count, parts, part_rows, width = g.shape
    n = share.shape[0] // 2
    return pl.pallas_call(
        functools.partial(last_kernel, count, parts // 2),
        out_shape=(jax.ShapeDtypeStruct(g.shape[1:], BF), jax.ShapeDtypeStruct((rows, width), BF)),
        in_specs=[ANY, ANY],
        out_specs=[ANY, ANY],
        scratch_shapes=[
            pltpu.VMEM((n, width), BF),
            pltpu.VMEM((n, width), BF),
            pltpu.VMEM((n, width), BF),
            pltpu.VMEM((n, width), BF),
            pltpu.VMEM((rows, width), BF),
            pltpu.SemaphoreType.DMA((3,)),
            pltpu.SemaphoreType.DMA((3,)),
            pltpu.SemaphoreType.DMA((3,)),
        ] + sum_scratch(count, parts, part_rows, width),
        compiler_params=pltpu.CompilerParams(collective_id=2, has_side_effects=True, vmem_limit_bytes=48 << 20),
        name="last",
    )(g, share)


def normalize(values):
    centred = values - jnp.mean(values, axis=-1, keepdims=True)
    scale = lax.rsqrt(jnp.mean(centred * centred, axis=-1, keepdims=True) + EPS)
    return centred * scale, scale


def norm_back(grad, normal, scale, gain):
    e = grad * gain
    return scale * (e - jnp.mean(e, axis=-1, keepdims=True) - normal * jnp.mean(e * normal, axis=-1, keepdims=True))


def packed(parts, dp, most):
    pieces, width = parts[0].shape[0], parts[0].shape[2]
    rows = sum(p.shape[1] for p in parts)
    count, part_rows = split_rows(rows, dp, most)
    pad = count * dp * part_rows - rows
    parts = [p.astype(BF) for p in parts]
    if pad:
        parts = parts + [jnp.zeros((pieces, pad, width), BF)]
    return jnp.concatenate(parts, axis=1).reshape(pieces, count, dp, part_rows, width)


def small_rows(rows, rows_pad):
    width = rows[0].shape[-1]
    rows = [jnp.broadcast_to(r, (PIECES, width)) for r in rows]
    rows = rows + [jnp.zeros((PIECES, width), F32)] * (rows_pad - len(rows))
    return jnp.stack(rows, axis=1)


def shards(layer_in, prompt_len, cont_len, w_qkv, b_qv, w_proj, b_proj, ln1_gain, ln1_bias,
           ln2_gain, ln2_bias, w_in, b_in, w_out, b_out, out_grad):
    rows, width = layer_in.shape
    blocks = rows // CLEN
    dp = lax.axis_size("dp")
    part = w_qkv.shape[2]
    t = lax.axis_index("tensor")
    g1, c1, g2, c2 = (v.astype(F32)[None] for v in (ln1_gain, ln1_bias, ln2_gain, ln2_bias))

    group = t * blocks + jnp.arange(blocks)
    conts = group - PROMPT // CLEN
    own_len = jnp.where(conts >= 0, cont_len[0][jnp.clip(conts, 0, CONT - 1)], 0)
    lens = jnp.concatenate([prompt_len, own_len]).astype(jnp.int32)

    bias_rows = [jnp.pad(b_qv[i : i + 1], ((0, 0), (r * part, width - (r + 1) * part))) for i in range(2) for r in range(PIECES)]
    small = jnp.concatenate(bias_rows + [jnp.zeros((8, width), BF), b_in[None], jnp.zeros((15, width), BF)], axis=0)
    (q, kp, vp, ko, vo, ctx, lse, attn_input, prompt_input, wq_all, wp_all, wi_all, wo_all, ws_all) = front_call(
        lens, layer_in, g1, c1, w_qkv.transpose(0, 2, 1), w_proj, w_in, w_out, small
    )

    w_proj_all = wp_all.reshape(width, width)
    rows_in = layer_in.astype(F32)
    hidden = rows_in + nn(ctx, w_proj_all) + b_proj.astype(F32)
    normal2, scale2 = normalize(hidden)
    mlp_input = (normal2 * g2 + c2).astype(BF)

    branch = 0.0
    grad_mlp_in = 0.0
    grad_in_pieces, grad_out_pieces, grad_b_in_pieces = [], [], []
    for r in range(PIECES):
        pre = nn(mlp_input, wi_all[r]) + ws_all[r, 16].astype(F32)
        cdf = 0.5 * (1.0 + lax.erf(pre * (0.5**0.5)))
        pdf = jnp.exp(-0.5 * pre * pre) * 0.3989422804014327
        gelu = (pre * cdf).astype(BF)
        branch = branch + nn(gelu, wo_all[r])
        grad_pre = (nt(out_grad, wo_all[r]) * (cdf + pre * pdf)).astype(BF)
        grad_out_pieces.append(tn(gelu, out_grad).astype(BF))
        grad_in_pieces.append(tn(mlp_input, grad_pre).astype(BF))
        grad_b_in_pieces.append(jnp.sum(grad_pre.astype(F32), axis=0))
        grad_mlp_in = grad_mlp_in + nt(grad_pre, wi_all[r])
    layer_out = (hidden + (branch + b_out.astype(F32))).astype(BF)

    dy = out_grad.astype(F32)
    grad_hidden = dy + norm_back(grad_mlp_in, normal2, scale2, g2)
    grad_attn = grad_hidden.astype(BF)
    sums = [
        jnp.stack(grad_b_in_pieces),
        jnp.sum(grad_attn.astype(F32), axis=0),
        jnp.sum(grad_mlp_in * normal2, axis=0),
        jnp.sum(grad_mlp_in, axis=0),
        jnp.sum(dy, axis=0),
    ]
    grad_ctx = nt(grad_attn, w_proj_all).astype(BF)
    grad_proj = tn(ctx, grad_attn).reshape(PIECES, part, width)
    g_first = packed([jnp.stack(grad_in_pieces), jnp.stack(grad_out_pieces), grad_proj, small_rows(sums, 16)], dp, 7)
    dq, dkp, dvp, dko, dvo, first = attn_bwd(lens, q, kp, vp, ko, vo, grad_ctx, ctx, lse, g_first)
    first = first.reshape(-1, width).astype(F32)
    hid = w_in.shape[1]
    grad_w_in, first = first[:width], first[width:]
    grad_w_out, first = first[:hid], first[hid:]
    grad_w_proj, first = first[:part], first[part:]

    grad_own_in = nn(dq, wq_all[0]) + nn(dko, wq_all[1]) + nn(dvo, wq_all[2])
    grad_prompt_in = nn(dkp, wq_all[1]) + nn(dvp, wq_all[2])
    gq = tn(dq, attn_input)
    gk = tn(dko, attn_input) + tn(dkp, prompt_input)
    gv = tn(dvo, attn_input) + tn(dvp, prompt_input)
    sum_q = jnp.sum(dq.astype(F32), axis=0).reshape(PIECES, part)
    sum_v = (jnp.sum(dvo.astype(F32), axis=0) + jnp.sum(dvp.astype(F32), axis=0)).reshape(PIECES, part)
    sum_qv = jnp.pad(jnp.concatenate([sum_q, sum_v], axis=1), ((0, 0), (0, width - 2 * part)))
    normal1, scale1 = normalize(rows_in)
    gain_off = prompt_input.astype(F32) - c1
    sum_g1 = jnp.sum(grad_own_in * normal1, axis=0) + jnp.sum(grad_prompt_in * gain_off, axis=0) / g1[0]
    sum_c1 = jnp.sum(grad_own_in, axis=0) + jnp.sum(grad_prompt_in, axis=0)
    g_last = packed(
        [v.reshape(PIECES, part, width) for v in (gq, gk, gv)] + [small_rows([sum_qv, sum_g1, sum_c1], 16)], dp, 5
    )
    last, extra = last_call(g_last, grad_prompt_in.astype(BF), rows)
    last = last.reshape(-1, width).astype(F32)
    grad_w_qkv = last[: 3 * part].reshape(3, part, width).transpose(0, 2, 1)
    last = last[3 * part :]
    grad_b_qv = last[0, : 2 * part].reshape(2, part)
    in_grad = grad_hidden + norm_back(grad_own_in + extra.astype(F32), normal1, scale1, g1)
    return (layer_out, in_grad, grad_w_qkv, grad_b_qv, grad_w_proj, first[1], last[1], last[2], first[2],
            first[3], grad_w_in, first[0, :hid], grad_w_out, first[4])


def solution(mesh):
    in_specs = (
        P(("dp", "tensor"), None),
        P("dp"),
        P("dp", None),
        P(None, None, "tensor"),
        P(None, "tensor"),
        P("tensor", None),
        P(),
        P(),
        P(),
        P(),
        P(),
        P(None, "tensor"),
        P("tensor"),
        P("tensor", None),
        P(),
        P(("dp", "tensor"), None),
    )
    out_specs = (
        P(("dp", "tensor"), None),
        P(("dp", "tensor"), None),
        P(None, None, "tensor"),
        P(None, "tensor"),
        P("tensor", None),
        P(),
        P(),
        P(),
        P(),
        P(),
        P(None, "tensor"),
        P("tensor"),
        P("tensor", None),
        P(),
    )
    return jax.shard_map(shards, mesh=mesh, in_specs=in_specs, out_specs=out_specs, check_vma=False)
```

time: 587 us -> 460 us (0.78)
  Pallas kernels: 97.8 us -> 280 us
  waiting for transfers between devices: 181 us -> 0 us
  blocking collectives: 70.7 us -> 0 us
  local copies, waits for them, and re-layouts: 27.3 us -> 90.2 us
  starting transfers between devices: 55 us -> 0 us
  matrix products: 99.5 us -> 65.1 us
  other arithmetic: 44.9 us -> 13.8 us
    pallas_call x4 -> x3, Pallas kernels: 97.8 us -> 280 us  [the longest x1 124 us: attn_bwd(): pl.pallas_call(functools.partial(attn_bwd_kernel, count, parts // 2), out...]
    ppermute x54 -> x0, waiting for transfers between devices: 181 us -> none  [the longest x51 154 us: swap(): lax.ppermute(v, axis, [(i, i ^ bit) for i in range(lax.axis_size(axis))])]
    psum x1 -> x0, blocking collectives: 70.7 us -> none  [shards(): small = lax.psum(small, ('dp', 'tensor'))]
    concatenate x3, local copies, waits for them, and re-layouts: 2.83 us -> 71.4 us  [the longest x2 71.2 us: packed(): jnp.concatenate(parts, axis=1).reshape(pieces, count, dp, part_rows, width)]
    ppermute x54 -> x0, starting transfers between devices: 55 us -> none  [the longest x51 48.3 us: swap(): lax.ppermute(v, axis, [(i, i ^ bit) for i in range(lax.axis_size(axis))])]
    dot_general x20 -> x9, matrix products: 39.7 us -> 16.2 us  [nt(): lax.dot_general(a, b, (((1,), (1,)), ((), ())), preferred_element_type=F32)]
    convert_element_type x34 -> x8, other arithmetic: 14.9 us -> 1.64 us  [the longest x1 0.69 us: shards(): first = first.reshape(-1, width).astype(F32)]
    dot_general x16 -> x14, matrix products: 31.2 us -> 19.7 us  [tn(): lax.dot_general(a, b, (((0,), (0,)), ((), ())), preferred_element_type=F32)]
  transfers between devices with their start and end apart: 54 -> 0, of which waited for: 28 -> 0; matrix products, arithmetic and copies ran while one was open for 21% -> 0% of each run, Pallas kernels for 6% -> 0%
where the time goes in v2:
time: 460 us; the launch traced here: 451 us
  Pallas kernels  280 us (61%)
  local copies, waits for them, and re-layouts  90.2 us (20%)
  matrix products  65.1 us (14%)
  other arithmetic  13.8 us (3%)
    pallas_call x1, Pallas kernels, attn_bwd(): pl.pallas_call(functools.partial(attn_bwd_kernel, count, parts // 2), out...  124 us
    pallas_call x1, Pallas kernels, front_call(): pl.pallas_call(front_kernel, out_shape=(shape(rows, width), shape(PROMPT,...  87.5 us
    concatenate x2, local copies, waits for them, and re-layouts, packed(): jnp.concatenate(parts, axis=1).reshape(pieces, count, dp, part_rows, width)  71.2 us
    pallas_call x1, Pallas kernels, last_call(): pl.pallas_call(functools.partial(last_kernel, count, parts // 2), out_sha...  68.7 us
    dot_general x14, matrix products, nn(): lax.dot_general(a, b, (((1,), (0,)), ((), ())), preferred_element_type=F32)  29.2 us
    dot_general x14, matrix products, tn(): lax.dot_general(a, b, (((0,), (0,)), ((), ())), preferred_element_type=F32)  19.7 us
    dot_general x9, matrix products, nt(): lax.dot_general(a, b, (((1,), (1,)), ((), ())), preferred_element_type=F32)  16.2 us

profile of v2, /device:TPU:0, one launch (start us, length us, event | category | flops | bytes accessed | tf_op | source)
XLA Modules:
  0.0 451.5 jit_solution(10670551879209211618)
XLA Ops:
  8.0 87.5 %front.1 = (bf16[768,768]{1,0:T(8,128)(2,1)S(1)}, bf16[1024,768]{1,0:T(8,128)(2,1)}, bf16[1024,768]{1,0:T(8,128)(2,1)}, bf16[768,768]{1,0:T(8,128)(2,1)S(1)}, bf...) custom-call(s32[4]{0:T(128)S(1)} %pad_add_fusion.lens, ...), custom_call_target="tpu_custom_call" | custom-call | flops 12079595520 | bytes 4194304 | tf_op jit(solution)/shard_map/front/pallas_call | solution.py:532
  95.6 4.1 fusion.113
  100.7 1.5 copy-done.21
  102.2 2.8 multiply_convert_fusion.1
  111.9 2.4 add_convert_fusion.2
  114.3 2.2 fusion.114
  116.4 2.2 fusion.115
  119.7 2.2 fusion.117
  123.1 2.4 fusion.116
  126.6 1.8 multiply_reduce_fusion.1
  128.4 1.3 convert_reduce_fusion.7
  130.5 1.3 copy-done.27
  131.8 2.2 convolution_convert_fusion.10.do_ref
  138.5 2.9 pad_maximum_fusion
  146.0 2.4 pad_maximum_fusion.1
  149.9 47.1 %concatenate.20 = bf16[4,1792,768]{2,1,0:T(8,128)(2,1)} concatenate(bf16[4,768,768]{2,1,0:T(8,128)(2,1)} %pad_maximum_fusion, bf16[4,768,768]{2,1,0:T(8,128)(2,1)} %pad_maximum_fusion.1, bf16[4,192,768]{2,1,0:T(8,128)(2,1)S(1)} %bitcast.179, bf16[4,1,768]{2,1,0:T(2,128)(2,1)S(1)} %copy.32, bf16[4,1,768]{2,1,0:T(2,128)(2,1)S(1)} %stack_broadcast_in_dim.18, ...), dimensions={1} | concatenate | bytes 22020096 | tf_op jit(solution)/shard_map/concatenate | solution.py:815
  196.9 123.8 %attn_bwd.1 = (bf16[768,768]{1,0:T(8,128)(2,1)}, bf16[1024,768]{1,0:T(8,128)(2,1)}, bf16[1024,768]{1,0:T(8,128)(2,1)}, bf16[768,768]{1,0:T(8,128)(2,1)}, bf16[76...) custom-call(s32[4]{0:T(128)} %copy-done.4, bf16[768,768]{1,0:T(8,128)(2,1)} %copy-done.5, ...), custom_call_target="tpu_custom_call" | custom-call | flops 30198988800 | bytes 15728640 | tf_op jit(solution)/shard_map/attn_bwd/pallas_call | solution.py:674
  320.8 2.9 fusion.50
  325.1 2.8 fusion.108
  328.0 2.1 convolution_convert_fusion
  330.1 1.5 fusion.118
  331.6 2.2 add_convert_fusion.1
  333.8 1.5 fusion.119
  335.3 2.2 add_convert_fusion
  338.5 3.3 fusion.46
  341.8 3.1 fusion.107
  345.0 24.1 %concatenate.22 = bf16[4,640,768]{2,1,0:T(8,128)(2,1)} concatenate(bf16[4,192,768]{2,1,0:T(8,128)(2,1)} %bitcast.180, bf16[4,192,768]{2,1,0:T(8,128)(2,1)} %bitcast.181, bf16[4,192,768]{2,1,0:T(8,128)(2,1)} %bitcast.182, bf16[4,1,768]{2,1,0:T(2,128)(2,1)S(1)} %copy.33, bf16[4,1,768]{2,1,0:T(2,128)(2,1)S(1)} %stack_broadcast_in_dim.22, ...), dimensions={1} | concatenate | bytes 7864320 | tf_op jit(solution)/shard_map/concatenate | solution.py:815
  369.1 68.7 %last.1 = (bf16[5,8,16,768]{3,2,1,0:T(8,128)(2,1)S(1)}, bf16[768,768]{1,0:T(8,128)(2,1)S(1)}) custom-call(bf16[4,5,8,16,768]{4,3,2,1,0:T(8,128)(2,1)} %bitcast.172, bf16[1024,768]{1,0:T(8,128)(2,1)S(1)} %get-tuple-element.81.share), custom_call_target="tpu_custom_call" | custom-call | tf_op jit(solution)/shard_map/last/pallas_call | solution.py:776
  439.4 2.1 fusion.9
  441.7 1.3 slice.158
  447.0 1.4 slice_reduce_fusion.4
  448.5 2.8 fusion.109
  (158 shorter events, 37.2 us)
Async XLA Ops:
  2.8 92.8 %copy-start.4 = (s32[4]{0:T(128)}, s32[4]{0:T(128)S(1)}, u32[]{:S(2)}) copy-start(s32[4]{0:T(128)S(1)} %pad_add_fusion.lens) | copy-start | bytes 52
  8.0 87.5 %copy-start.9 = (bf16[768,768]{1,0:T(8,128)(2,1)S(1)}, bf16[768,768]{1,0:T(8,128)(2,1)}, u32[]{:S(2)}) copy-start(bf16[768,768]{1,0:T(8,128)(2,1)} %x_ref.1) | copy-start | bytes 3538948
  95.5 4.2 copy-start.5
  95.5 4.2 copy-start.6
  95.5 4.2 copy-start.7
  95.6 4.2 copy-start.8
  95.6 4.2 copy-start.24
  95.6 4.2 copy-start.25
  99.9 2.3 copy-start.21
  100.3 4.7 %slice-start = ((s8[4718592]{0:T(1024)(128)(4,1)}), s8[4194304]{0:T(1024)(128)(4,1)S(1)}, s32[]{:S(2)}) async-start(s8[4718592]{0:T(1024)(128)(4,1)} %bitcast.183), calls=%async_computation | async-start | bytes 8388608
  102.2 2.8 slice-start.1
  111.9 2.4 copy-start.18
  114.3 2.2 copy-start.33
  128.4 1.3 copy-start.22
  129.7 18.8 %copy-start.12 = (f32[768,768]{1,0:T(8,128)}, f32[768,768]{1,0:T(8,128)S(1)}, u32[]{:S(2)}) copy-start(f32[768,768]{1,0:T(8,128)S(1)} %get-tuple-element.80) | copy-start | bytes 7077892
  129.7 2.1 copy-start.27
  146.0 2.5 copy-start.34
  320.8 2.9 copy-start.20
  320.8 3.0 copy-start.30
  323.8 1.3 copy-start.15
  325.1 2.8 copy-start.19
  325.1 2.8 copy-start.32
  328.0 2.2 copy-start.28
  328.0 2.2 copy-start.31
  331.6 2.2 copy-start.16
  338.5 3.3 copy-start.17
  338.5 3.3 copy-start.29
  369.1 68.7 %copy-start.10 = (f32[768,768]{1,0:T(8,128)S(1)}, f32[768,768]{1,0:T(8,128)}, u32[]{:S(2)}) copy-start(f32[768,768]{1,0:T(8,128)} %get-tuple-element.112) | copy-start | bytes 7077892
  437.8 1.7 copy-start.13
  441.7 1.9 copy-start.14
  441.7 3.1 copy-start.11
  448.5 2.8 copy-start.1
  (5 other events, 5.0 us)
